TPU v7x, 32 devices: a whole 2x2x4 slice. The times are simulated.
32 devices in a mesh: ctx: 8 (over z, x), exp: 4 (over y, core).
Axes of the slice: x: 2, y: 2, z: 4, core: 2. Of those that a mesh axis runs over, the one named last changes fastest.
Arguments:
- queries: bfloat16 [1024, 4096], P('ctx', 'exp'), may hold values from -5 to 5
- keys: bfloat16 [1024, 1024], P('ctx', 'exp'), may hold values from -5 to 5
- values: bfloat16 [1024, 1024], P('ctx', 'exp'), may hold values from -6 to 6
- resid_in: bfloat16 [1024, 4096], P(('ctx', 'exp')), may hold values from -6 to 6
- span_order: int32 [16], replicated, may hold values from 0 to 15, each once
- out_weight: bfloat16 [4096, 4096], P('exp'), may hold values from -0.09375 to 0.09375
- norm_gain: float32 [4096], replicated, may hold values from 0.25 to 1.75
- router: float32 [4096, 4], replicated, may hold values from -0.09375 to 0.09375
- expert_ids: int32 [1024, 2], P(('ctx', 'exp')), may hold values from 0 to 3, all different within a row; in each aligned block of 32 rows (0 to 31, 32 to 63, ...) at most 16 rows name the same one
- w_gate: bfloat16 [4, 4096, 14336], P('exp', None, 'ctx'), may hold values from -0.09375 to 0.09375
- w_up: bfloat16 [4, 4096, 14336], P('exp', None, 'ctx'), may hold values from -0.09375 to 0.09375
- w_down: bfloat16 [4, 14336, 4096], P('exp', 'ctx'), may hold values from -0.046875 to 0.046875
Outputs:
- mixed: bfloat16 [1024, 4096], P(('ctx', 'exp'))
Inputs may be any that keep to these rules, and one draw needn't show every extreme that they name: `expert_ids`: A token's 2 ids differ. In every aligned block of 32 tokens, each of the 4 experts is named by exactly 16 tokens. `span_order`: each span number appears once.
All inputs are finite; a program needn't handle non-finite values.
Results may differ from a plain program's by a relative error of at most 0.012.
Values may be sent and summed in bfloat16 or wider, within the bound.
A program may use at most 128 MiB of HBM per device.

v0:
```python
import functools
import math

import jax
import jax.numpy as jnp
from jax import lax
from jax.experimental import pallas as pl
from jax.experimental.pallas import tpu as pltpu
from jax.sharding import PartitionSpec as P

HEAD_SIZE = 128
SPAN = 64


def true_positions(row_ids, span_order):
    span_ids = jnp.arange(span_order.shape[0], dtype=jnp.int32)
    matches = (row_ids // SPAN)[:, None] == span_ids[None, :]
    return jnp.sum(jnp.where(matches, span_order[None, :], 0), axis=1) * SPAN + row_ids % SPAN


def on_device_xla(
    queries,
    keys,
    values,
    resid_in,
    span_order,
    out_weight,
    norm_gain,
    router,
    expert_ids,
    w_gate,
    w_up,
    w_down,
):
    tok_rows = queries.shape[0]
    kv_heads = keys.shape[1] // HEAD_SIZE
    head_cluster = queries.shape[1] // HEAD_SIZE // kv_heads
    ctx_index = lax.axis_index("ctx")
    query_pos = true_positions(
        ctx_index * tok_rows + jnp.arange(tok_rows, dtype=jnp.int32), span_order
    )
    shaped_queries = queries.reshape(tok_rows, kv_heads, head_cluster, HEAD_SIZE)
    score_scale = 1.0 / math.sqrt(HEAD_SIZE)
    pieces = (
        lax.all_gather(keys, "ctx", axis=0, tiled=True),
        lax.all_gather(values, "ctx", axis=0, tiled=True),
    )
    key_pos = true_positions(jnp.arange(pieces[0].shape[0], dtype=jnp.int32), span_order)
    running_max = jnp.full((kv_heads, head_cluster, tok_rows), -1e30, jnp.float32)
    key_block, value_block = pieces
    key_count = key_block.shape[0]
    key_head_rows = key_block.reshape(key_count, kv_heads, HEAD_SIZE)
    value_head_rows = value_block.reshape(key_count, kv_heads, HEAD_SIZE)
    scores = jnp.einsum(
        "qhgd,khd->hgqk", shaped_queries, key_head_rows, preferred_element_type=jnp.float32
    )
    allowed = key_pos[None, :] <= query_pos[:, None]
    scores = jnp.where(allowed[None, None], scores * score_scale, -1e30)
    new_max = jnp.maximum(running_max, jnp.max(scores, axis=-1))
    weights = jnp.where(allowed[None, None], jnp.exp(scores - new_max[..., None]), 0.0)
    running_sum = jnp.sum(weights, axis=-1)
    update = jnp.einsum(
        "hgqk,khd->qhgd",
        weights.astype(jnp.bfloat16),
        value_head_rows,
        preferred_element_type=jnp.float32,
    )
    weighted = update
    running_max, running_sum, weighted = (new_max, running_sum, weighted)
    attended = (
        (weighted / jnp.transpose(running_sum, (2, 0, 1))[..., None])
        .astype(jnp.bfloat16)
        .reshape(tok_rows, -1)
    )
    projected = jnp.dot(attended, out_weight, preferred_element_type=jnp.float32)
    own_sum = lax.psum_scatter(
        projected.astype(jnp.bfloat16), "exp", scatter_dimension=0, tiled=True
    ).astype(jnp.float32)
    stream = (resid_in.astype(jnp.float32) + own_sum).astype(jnp.bfloat16)
    stream_wide = stream.astype(jnp.float32)
    mean_square = jnp.mean(stream_wide * stream_wide, axis=-1, keepdims=True)
    normed = (stream_wide * lax.rsqrt(mean_square + 1e-05) * norm_gain).astype(jnp.bfloat16)
    model_dim = normed.shape[1]
    logits = jnp.dot(normed.astype(jnp.float32), router, precision=lax.Precision.HIGHEST)
    experts = router.shape[1]
    expert_axis = jnp.arange(experts, dtype=jnp.int32)
    picked = expert_ids[:, :, None] == expert_axis[None, None, :]
    chosen = jnp.sum(jnp.where(picked, logits[:, None, :], 0.0), axis=-1)
    mixing = jax.nn.softmax(chosen, axis=-1)
    token_weight = jnp.sum(jnp.where(picked, mixing[:, :, None], 0.0), axis=1)
    routed = jnp.any(picked, axis=1)
    rank_of = jnp.cumsum(routed.astype(jnp.int32), axis=0) - 1
    slot_count = resid_in.shape[0] * expert_ids.shape[1] // experts
    slot_axis = jnp.arange(slot_count, dtype=jnp.int32)
    placing = jnp.logical_and(
        routed.T[:, None, :], rank_of.T[:, None, :] == slot_axis[None, :, None]
    )
    outgoing = jnp.einsum(
        "est,td->esd", placing.astype(jnp.bfloat16), normed, preferred_element_type=jnp.float32
    ).astype(jnp.bfloat16)
    arrived = lax.all_to_all(outgoing, "exp", split_axis=0, concat_axis=0, tiled=True)
    rows_in = lax.all_gather(arrived.reshape(-1, model_dim), "ctx", axis=0, tiled=True)
    gate_part = jnp.dot(rows_in, w_gate[0], preferred_element_type=jnp.float32)
    up_part = jnp.dot(rows_in, w_up[0], preferred_element_type=jnp.float32)
    hidden = (jax.nn.silu(gate_part) * up_part).astype(jnp.bfloat16)
    partials = jnp.dot(hidden, w_down[0], preferred_element_type=jnp.float32)
    own_rows = lax.psum_scatter(
        partials.astype(jnp.bfloat16), "ctx", scatter_dimension=0, tiled=True
    )
    results = own_rows.reshape(experts, slot_count, model_dim)
    returned = lax.all_to_all(results, "exp", split_axis=0, concat_axis=0, tiled=True)
    coefficient = placing.astype(jnp.float32) * token_weight.T[:, None, :]
    combined = jnp.einsum("est,esd->td", coefficient, returned.astype(jnp.float32))
    return (stream_wide + combined).astype(jnp.bfloat16)


VMEM_BYTES = 60 * 2**20
LOAD_ROWS = 512
MESH = pl.DeviceIdType.MESH


def place_of():
    ctx, exp = lax.axis_index("ctx"), lax.axis_index("exp")
    return ctx // 2, ctx % 2, exp // 2, exp % 2


def at(z, x, y, c):
    return (z * 2 + x, y * 2 + c)


def greet(devices):
    barrier = pltpu.get_barrier_semaphore()
    for device in devices:
        pl.semaphore_signal(barrier, inc=1, device_id=device, device_id_type=MESH)
    pl.semaphore_wait(barrier, len(devices))


def start_send(src, dst, send_sem, recv_sem, device):
    copy = pltpu.make_async_remote_copy(
        src_ref=src,
        dst_ref=dst,
        send_sem=send_sem,
        recv_sem=recv_sem,
        device_id=device,
        device_id_type=MESH,
    )
    copy.start()
    return copy


def gather_keys_kernel(levels, k_ref, v_ref, ko_ref, vo_ref, zs, zr, xs, xr):
    z, x, y, c = place_of()
    greet([at((z + d) % levels, x, y, c) for d in range(1, levels)] + [at(z, 1 - x, y, c)])
    x_peer = at(z, 1 - x, y, c)
    mine = z * 2 + x
    z_copies, x_copies = [], []
    pairs = ((k_ref, ko_ref), (v_ref, vo_ref))
    for d in range(1, levels):
        for i, (own, out) in enumerate(pairs):
            z_copies.append(
                start_send(own, out.at[mine], zs.at[i, d], zr.at[i, d], at((z + d) % levels, x, y, c))
            )
    for i, (own, out) in enumerate(pairs):
        x_copies.append(start_send(own, out.at[mine], xs.at[i, 0], xr.at[i, 0], x_peer))
    for own, out in pairs:
        out[mine] = own[...]
    for d in range(1, levels):
        block = (z + levels - d) % levels * 2 + x
        for i, (own, out) in enumerate(pairs):
            z_copies[(d - 1) * 2 + i].wait_recv()
            x_copies.append(
                start_send(out.at[block], out.at[block], xs.at[i, d], xr.at[i, d], x_peer)
            )
    for copy in x_copies:
        copy.wait_recv()
    for copy in z_copies + x_copies:
        copy.wait_send()


def gather_keys(keys, values, levels):
    shape = jax.ShapeDtypeStruct((levels * 2,) + keys.shape, keys.dtype)
    vmem = pl.BlockSpec(memory_space=pltpu.VMEM)
    sems = pltpu.SemaphoreType.DMA((2, levels))
    return pl.pallas_call(
        functools.partial(gather_keys_kernel, levels),
        out_shape=(shape, shape),
        in_specs=[vmem] * 2,
        out_specs=(vmem, vmem),
        scratch_shapes=[sems] * 4,
        compiler_params=pltpu.CompilerParams(collective_id=0, has_side_effects=True),
    )(keys, values)


def stream_kernel(
    levels, sub, model, half, experts, slots, tile, proj_ref, resid_ref, gain_ref, router_ref,
    ids_ref, gate_ref, up_ref, stream_ref, hidden_ref, placing_ref, weight_ref,
    out_ref, gate_w, up_w, rows_ref,
    kept, from_core, from_y, ss, rs, zs, zr, xs, xr, ys, yr, ds, dr, es, er, cs, cr, gs, us,
):
    loads = []
    for part in range(model // LOAD_ROWS):
        rows = slice(part * LOAD_ROWS, (part + 1) * LOAD_ROWS)
        loads.append(pltpu.make_async_copy(gate_ref.at[0, rows], gate_w.at[rows], gs.at[part]))
        loads.append(pltpu.make_async_copy(up_ref.at[0, rows], up_w.at[rows], us.at[part]))
    for load in loads:
        load.start()
    z, x, y, c = place_of()
    x_peer, y_peer, c_peer = at(z, 1 - x, y, c), at(z, x, 1 - y, c), at(z, x, y, 1 - c)
    z_peers = [at((z + d) % levels, x, y, c) for d in range(1, levels)]
    greet(z_peers + [x_peer, y_peer, c_peer])

    order = (1 - y, y)
    first = [
        start_send(proj_ref.at[row, 1 - c], from_core.at[i], ss.at[i], rs.at[i], c_peer)
        for i, row in enumerate(order)
    ]
    first[0].wait_recv()
    kept[0] = (
        proj_ref[1 - y, c].astype(jnp.float32) + from_core[0].astype(jnp.float32)
    ).astype(jnp.bfloat16)
    second = start_send(kept.at[0], from_y, ss.at[2], rs.at[2], y_peer)
    first[1].wait_recv()
    total = proj_ref[y, c].astype(jnp.float32) + from_core[1].astype(jnp.float32)
    total = total + resid_ref[...].astype(jnp.float32)
    second.wait_recv()
    stream = (total + from_y[...].astype(jnp.float32)).astype(jnp.bfloat16)
    stream_ref[...] = stream
    wide = stream.astype(jnp.float32)
    mean_square = jnp.mean(wide * wide, axis=-1, keepdims=True)
    normed = (wide * lax.rsqrt(mean_square + 1e-05) * gain_ref[...]).astype(jnp.bfloat16)

    normed_wide = normed.astype(jnp.float32)
    logits = [
        jnp.sum(normed_wide * router_ref[e : e + 1, :], axis=-1, keepdims=True)
        for e in range(experts)
    ]
    ids = ids_ref[...]
    id0, id1 = ids[:, 0:1], ids[:, 1:2]
    zero = jnp.zeros_like(logits[0])
    pick0, pick1 = zero, zero
    for e in range(experts):
        pick0 = pick0 + jnp.where(id0 == e, logits[e], 0.0)
        pick1 = pick1 + jnp.where(id1 == e, logits[e], 0.0)
    top = jnp.maximum(pick0, pick1)
    exp0, exp1 = jnp.exp(pick0 - top), jnp.exp(pick1 - top)
    gate0, gate1 = exp0 / (exp0 + exp1), exp1 / (exp0 + exp1)
    lane = lax.broadcasted_iota(jnp.int32, (sub, 128), 1)
    expert = lane % experts
    routed = jnp.logical_or(expert == id0, expert == id1)
    weight = jnp.where(expert == id0, gate0, 0.0) + jnp.where(expert == id1, gate1, 0.0)
    high = weight.astype(jnp.bfloat16).astype(jnp.float32)
    group = lane // experts
    tail = jnp.where(
        group == 0,
        jnp.where(routed, 1.0, 0.0),
        jnp.where(group == 1, high, jnp.where(group == 2, weight - high, 0.0)),
    )

    def block(k, bx, by):
        return ((k * 2 + bx) * 2 + by) * 2 + c

    mine = block(z, x, y)
    out_ref[mine, :, 0:model] = normed
    out_ref[mine, :, model : model + 128] = tail.astype(jnp.bfloat16)

    left, right = slice(0, half), slice(half, model + 128)
    copies = [second] + first
    own = out_ref.at[mine]
    z_copies = [None] + [
        start_send(own, own, zs.at[d], zr.at[d], z_peers[d - 1]) for d in range(1, levels)
    ]
    x_copies, y_copies, d_copies, e_copies, c_copies = [], [], [], [], []

    def to_core(index):
        n = len(c_copies)
        ref = out_ref.at[index]
        c_copies.append(start_send(ref, ref, cs.at[n], cr.at[n], c_peer))
        return n

    sent = {d: [] for d in range(levels)}

    def finish(d):
        k = (z + levels - d) % levels
        d_copies[d].wait_recv()
        e_copies[d].wait_recv()
        sent[d].append(to_core(block(k, 1 - x, 1 - y)))

    mine_expert = lax.axis_index("exp")
    count = 8 * sub

    def experts_of(d):
        k = (z + levels - d) % levels
        for n in sent[d]:
            c_copies[n].wait_recv()
        info = out_ref[pl.ds(k * 8, 8), :, model : model + 128].reshape(count, 128)
        above = lax.broadcasted_iota(jnp.int32, (count, count), 0)
        below = lax.broadcasted_iota(jnp.int32, (count, count), 1)
        within = jnp.logical_and(above // sub == below // sub, below <= above)
        seen = jnp.dot(
            jnp.where(within, 1.0, 0.0).astype(jnp.bfloat16),
            info,
            preferred_element_type=jnp.float32,
        )
        wide_info = info.astype(jnp.float32)
        at_lane = lax.broadcasted_iota(jnp.int32, (count, 128), 1)

        def lane_sum(value, keep):
            return jnp.sum(jnp.where(keep, value, 0.0), axis=1, keepdims=True)

        is_mine = at_lane == mine_expert
        here = lane_sum(wide_info, is_mine)
        rank = lane_sum(seen, is_mine).astype(jnp.int32) - 1
        token_weight = lane_sum(
            wide_info,
            jnp.logical_or(at_lane == experts + mine_expert, at_lane == 2 * experts + mine_expert),
        )
        token = lax.broadcasted_iota(jnp.int32, (count, 1), 0)
        slot = jnp.where(here > 0.5, token // sub * slots + rank, -1)
        at_slot = lax.broadcasted_iota(jnp.int32, (count, 8 * slots), 1)
        placing = jnp.where(at_slot == slot, 1.0, 0.0).astype(jnp.bfloat16)
        placing_ref[k] = placing
        weight_ref[k] = jnp.broadcast_to(token_weight, (count, 128))
        picked_rows = jnp.where(at_slot == slot, 1.0, 0.0).T.astype(jnp.bfloat16)

        def pick(j, carry):
            columns = pl.ds(pl.multiple_of(j * 512, 512), 512)
            block_in = out_ref[pl.ds(k * 8, 8), :, columns].reshape(count, 512)
            rows_ref[:, columns] = jnp.dot(
                picked_rows, block_in, preferred_element_type=jnp.float32
            ).astype(jnp.bfloat16)
            return carry

        lax.fori_loop(0, model // 512, pick, 0)
        if d == 0:
            for load in loads:
                load.wait()

        def unit(j, carry):
            columns = pl.ds(pl.multiple_of(j * tile, tile), tile)
            rows = rows_ref[...]
            gate = jnp.dot(rows, gate_w[:, columns], preferred_element_type=jnp.float32)
            up = jnp.dot(rows, up_w[:, columns], preferred_element_type=jnp.float32)
            hidden_ref[k, :, columns] = (gate * jax.nn.sigmoid(gate) * up).astype(jnp.bfloat16)
            return carry

        lax.fori_loop(0, hidden_ref.shape[2] // tile, unit, 0)

    for turn in range(levels + 1):
        if turn < levels:
            k = (z + levels - turn) % levels
            if turn:
                z_copies[turn].wait_recv()
            ref = out_ref.at[block(k, x, y)]
            x_copies.append(start_send(ref, ref, xs.at[turn], xr.at[turn], x_peer))
            y_copies.append(start_send(ref, ref, ys.at[turn], yr.at[turn], y_peer))
            sent[turn].append(to_core(block(k, x, y)))
        if turn:
            d = turn - 1
            k = (z + levels - d) % levels
            x_copies[d].wait_recv()
            ref = out_ref.at[block(k, 1 - x, y), :, left]
            d_copies.append(start_send(ref, ref, ds.at[d], dr.at[d], y_peer))
            sent[d].append(to_core(block(k, 1 - x, y)))
            y_copies[d].wait_recv()
            ref = out_ref.at[block(k, x, 1 - y), :, right]
            e_copies.append(start_send(ref, ref, es.at[d], er.at[d], x_peer))
            sent[d].append(to_core(block(k, x, 1 - y)))
        if turn >= 2:
            finish(turn - 2)
            experts_of(turn - 2)
    finish(levels - 1)
    experts_of(levels - 1)
    for copy in copies + z_copies[1:] + x_copies + y_copies + d_copies + e_copies + c_copies:
        copy.wait_send()


def stream_and_hidden(projected, resid_in, norm_gain, router, expert_ids, gate, up, levels):
    sub, model = resid_in.shape
    experts = router.shape[1]
    width = gate.shape[2]
    slots = sub * expert_ids.shape[1] // experts
    vmem = pl.BlockSpec(memory_space=pltpu.VMEM)
    hbm = pl.BlockSpec(memory_space=pl.ANY)
    dma = pltpu.SemaphoreType.DMA
    bf16 = jnp.bfloat16
    return pl.pallas_call(
        functools.partial(
            stream_kernel, levels, sub, model, model // 2, experts, slots, width // 7
        ),
        out_shape=(
            jax.ShapeDtypeStruct((sub, model), bf16),
            jax.ShapeDtypeStruct((levels, 8 * slots, width), bf16),
            jax.ShapeDtypeStruct((levels, 8 * sub, 8 * slots), bf16),
            jax.ShapeDtypeStruct((levels, 8 * sub, 128), jnp.float32),
        ),
        in_specs=[vmem] * 5 + [hbm] * 2,
        out_specs=(vmem,) * 4,
        scratch_shapes=[
            pltpu.VMEM((levels * 8, sub, model + 128), bf16),
            pltpu.VMEM((model, width), bf16),
            pltpu.VMEM((model, width), bf16),
            pltpu.VMEM((8 * slots, model), bf16),
            pltpu.VMEM((1, sub, model), bf16),
            pltpu.VMEM((2, sub, model), bf16),
            pltpu.VMEM((sub, model), bf16),
            dma((3,)),
            dma((3,)),
        ]
        + [dma((levels,))] * 10
        + [dma((levels * 4,))] * 2
        + [dma((model // LOAD_ROWS,))] * 2,
        compiler_params=pltpu.CompilerParams(
            collective_id=1, has_side_effects=True, vmem_limit_bytes=VMEM_BYTES
        ),
    )(
        projected.reshape(2, 2, sub, model),
        resid_in,
        norm_gain.reshape(1, model),
        router.T,
        expert_ids,
        gate,
        up,
    )


def sum_kernel(
    levels, sub, model, half, tile, hidden_ref, placing_ref, weight_ref, down_ref, stream_ref,
    out_ref, part_ref, down_w, core_in, held, a_in, b_in, a2_in, b2_in, ready, z_in,
    cs, cr, sa, ra, sb, rb, sa2, ra2, sb2, rb2, zs, zr, ls,
):
    loads = []
    for j in range(model // tile):
        columns = slice(j * tile, (j + 1) * tile)
        loads.append(
            pltpu.make_async_copy(down_ref.at[0, :, columns], down_w.at[:, columns], ls.at[j])
        )
        loads[j].start()
    z, x, y, c = place_of()
    x_peer, y_peer, c_peer = at(z, 1 - x, y, c), at(z, x, 1 - y, c), at(z, x, y, 1 - c)
    z_peers = [at((z + d) % levels, x, y, c) for d in range(1, levels)]
    greet(z_peers + [x_peer, y_peer, c_peer])
    turns = list(range(1, levels)) + [0]
    left, right = slice(0, half), slice(half, model)
    f32, bf16 = jnp.float32, jnp.bfloat16
    c_copies = [None] * levels

    def terms_of(d):
        k = (z + d) % levels
        lanes = weight_ref[k]
        weight = jnp.concatenate([lanes] * (tile // 128), axis=1)
        hidden = hidden_ref[k]
        placing = placing_ref[k]

        def one(columns):
            rows = jnp.dot(hidden, down_w[:, columns], preferred_element_type=f32).astype(bf16)
            spread = jnp.dot(placing, rows, preferred_element_type=f32)
            part_ref[k, :, :, :, :, columns] = (
                (spread * weight).astype(bf16).reshape(2, 2, 2, sub, tile)
            )

        if d == turns[0]:
            for j in range(model // tile):
                loads[j].wait()
                one(slice(j * tile, (j + 1) * tile))
        else:

            def looped(j, carry):
                one(pl.ds(pl.multiple_of(j * tile, tile), tile))
                return carry

            lax.fori_loop(0, model // tile, looped, 0)
        c_copies[d] = start_send(
            part_ref.at[k, :, :, 1 - c], core_in.at[d], cs.at[d], cr.at[d], c_peer
        )
    terms_of(turns[0])
    stage2, stage3, z_copies = {}, {}, {}
    for step in range(levels + 2):
        if step < levels:
            d = turns[step]
            k = (z + d) % levels
            c_copies[d].wait_recv()
            for bx in range(2):
                for by in range(2):
                    held[d, bx, by] = (
                        part_ref[k, bx, by, c].astype(f32) + core_in[d, bx, by].astype(f32)
                    ).astype(bf16)
            stage2[d] = (
                start_send(
                    held.at[d, :, 1 - y, :, left], a_in.at[d], sa.at[d], ra.at[d], y_peer
                ),
                start_send(
                    held.at[d, 1 - x, :, :, right], b_in.at[d], sb.at[d], rb.at[d], x_peer
                ),
            )
        if step + 1 < levels:
            terms_of(turns[step + 1])
        if 1 <= step <= levels:
            d = turns[step - 1]
            stage2[d][0].wait_recv()
            ready[d, :, left] = (
                held[d, 1 - x, y, :, left].astype(f32) + a_in[d, 1 - x].astype(f32)
            ).astype(bf16)
            stage2[d][1].wait_recv()
            ready[d, :, right] = (
                held[d, x, 1 - y, :, right].astype(f32) + b_in[d, 1 - y].astype(f32)
            ).astype(bf16)
            stage3[d] = (
                start_send(ready.at[d, :, left], a2_in.at[d], sa2.at[d], ra2.at[d], x_peer),
                start_send(ready.at[d, :, right], b2_in.at[d], sb2.at[d], rb2.at[d], y_peer),
            )
        if step >= 2:
            d = turns[step - 2]
            stage3[d][0].wait()
            stage3[d][1].wait()
            low = (
                held[d, x, y, :, left].astype(f32)
                + a_in[d, x].astype(f32)
                + a2_in[d].astype(f32)
            )
            high = (
                held[d, x, y, :, right].astype(f32)
                + b_in[d, y].astype(f32)
                + b2_in[d].astype(f32)
            )
            if d:
                ready[d, :, left] = low.astype(bf16)
                ready[d, :, right] = high.astype(bf16)
                z_copies[d] = start_send(
                    ready.at[d], z_in.at[d], zs.at[d], zr.at[d], z_peers[d - 1]
                )
            else:
                for d in range(1, levels):
                    z_copies[d].wait_recv()
                    low = low + z_in[d, :, left].astype(f32)
                    high = high + z_in[d, :, right].astype(f32)
                out_ref[:, left] = (stream_ref[:, left].astype(f32) + low).astype(bf16)
                out_ref[:, right] = (stream_ref[:, right].astype(f32) + high).astype(bf16)
    for d in range(levels):
        c_copies[d].wait_send()
        for copy in stage2[d]:
            copy.wait_send()
        if d:
            z_copies[d].wait_send()


def sum_terms(hidden, placing, weight, down, stream, levels):
    sub, model = stream.shape
    half = model // 2
    tile = 512
    vmem = pl.BlockSpec(memory_space=pltpu.VMEM)
    dma = pltpu.SemaphoreType.DMA
    bf16 = jnp.bfloat16
    return pl.pallas_call(
        functools.partial(sum_kernel, levels, sub, model, half, tile),
        out_shape=jax.ShapeDtypeStruct((sub, model), bf16),
        in_specs=[vmem] * 3 + [pl.BlockSpec(memory_space=pl.ANY), vmem],
        out_specs=vmem,
        scratch_shapes=[
            pltpu.VMEM((levels, 2, 2, 2, sub, model), bf16),
            pltpu.VMEM(down.shape[1:], bf16),
            pltpu.VMEM((levels, 2, 2, sub, model), bf16),
            pltpu.VMEM((levels, 2, 2, sub, model), bf16),
            pltpu.VMEM((levels, 2, sub, half), bf16),
            pltpu.VMEM((levels, 2, sub, half), bf16),
            pltpu.VMEM((levels, sub, half), bf16),
            pltpu.VMEM((levels, sub, half), bf16),
            pltpu.VMEM((levels, sub, model), bf16),
            pltpu.VMEM((levels, sub, model), bf16),
        ]
        + [dma((levels,))] * 12
        + [dma((model // tile,))],
        compiler_params=pltpu.CompilerParams(
            collective_id=2, has_side_effects=True, vmem_limit_bytes=VMEM_BYTES
        ),
    )(hidden, placing, weight, down, stream)


def on_device(
    levels,
    queries,
    keys,
    values,
    resid_in,
    span_order,
    out_weight,
    norm_gain,
    router,
    expert_ids,
    w_gate,
    w_up,
    w_down,
):
    tok_rows = queries.shape[0]
    kv_heads = keys.shape[1] // HEAD_SIZE
    head_cluster = queries.shape[1] // HEAD_SIZE // kv_heads
    ctx_index = lax.axis_index("ctx")
    query_pos = true_positions(
        ctx_index * tok_rows + jnp.arange(tok_rows, dtype=jnp.int32), span_order
    )
    shaped_queries = queries.reshape(tok_rows, kv_heads, head_cluster, HEAD_SIZE)
    score_scale = 1.0 / math.sqrt(HEAD_SIZE)
    all_keys, all_values = gather_keys(keys, values, levels)
    key_count = levels * 2 * tok_rows
    key_pos = true_positions(jnp.arange(key_count, dtype=jnp.int32), span_order)
    key_head_rows = all_keys.reshape(key_count, kv_heads, HEAD_SIZE)
    value_head_rows = all_values.reshape(key_count, kv_heads, HEAD_SIZE)
    scores = jnp.einsum(
        "qhgd,khd->hgqk", shaped_queries, key_head_rows, preferred_element_type=jnp.float32
    )
    allowed = key_pos[None, :] <= query_pos[:, None]
    scores = jnp.where(allowed[None, None], scores * score_scale, -1e30)
    row_max = jnp.max(scores, axis=-1)
    weights = jnp.where(allowed[None, None], jnp.exp(scores - row_max[..., None]), 0.0)
    row_sum = jnp.sum(weights, axis=-1)
    weighted = jnp.einsum(
        "hgqk,khd->qhgd",
        weights.astype(jnp.bfloat16),
        value_head_rows,
        preferred_element_type=jnp.float32,
    )
    attended = (
        (weighted / jnp.transpose(row_sum, (2, 0, 1))[..., None])
        .astype(jnp.bfloat16)
        .reshape(tok_rows, -1)
    )
    projected = jnp.dot(attended, out_weight, preferred_element_type=jnp.float32).astype(
        jnp.bfloat16
    )
    stream, hidden, placing, weight = stream_and_hidden(
        projected, resid_in, norm_gain, router, expert_ids, w_gate, w_up, levels
    )
    return sum_terms(hidden, placing, weight, w_down, stream, levels)


def solution(mesh):
    placed = (
        P("ctx", "exp"),
        P("ctx", "exp"),
        P("ctx", "exp"),
        P(("ctx", "exp"), None),
        P(),
        P("exp", None),
        P(),
        P(),
        P(("ctx", "exp"), None),
        P("exp", None, "ctx"),
        P("exp", None, "ctx"),
        P("exp", "ctx", None),
    )
    levels = mesh.shape["ctx"] // 2

    def body(queries, keys, values, resid_in, *rest):
        blocks = resid_in.size * mesh.size * 2
        small = mesh.shape["exp"] == 4 and mesh.shape["ctx"] % 2 == 0 and blocks * 4 <= VMEM_BYTES
        local = functools.partial(on_device, levels) if small else on_device_xla
        return local(queries, keys, values, resid_in, *rest)

    return jax.shard_map(
        body, mesh=mesh, in_specs=placed, out_specs=P(("ctx", "exp"), None), check_vma=False
    )
```

profile of v0, /device:TPU:0, one launch (start us, length us, event | category | flops | bytes accessed | tf_op | source)
XLA Modules:
  0.0 177.3 jit_solution(793142513874350249)
XLA Ops:
  0.0 0.7 select_reduce_fusion.1
  0.8 0.7 select_reduce_fusion
  1.5 0.2 broadcast_compare_fusion
  1.7 23.3 %shard_map.118 = (bf16[8,128,256]{2,1,0:T(8,128)(2,1)}, bf16[8,128,256]{2,1,0:T(8,128)(2,1)}) custom-call(bf16[128,256]{1,0:T(8,128)(2,1)} %k_ref.1, bf16[128,256]{1,0:T(8,128)(2,1)} %v_ref.1), custom_call_target="tpu_custom_call" | custom-call | tf_op jit(solution)/shard_map/pallas_call | solution.py:184
  25.0 1.2 reshape.111
  26.2 1.1 reshape.112
  27.3 0.7 fusion.16
  28.0 0.0 copy-start
  28.1 2.3 %fusion.31 = (f32[2,4,128]{2,1,0:T(4,128)S(1)}, bf16[2,4,128,1024]{2,3,1,0:T(8,128)(2,1)S(1)}) fusion(f32[2,1024,128,4]{2,1,3,0:T(8,128)S(1)} %fusion.16, pred[128,1024]{0,1:T(8,128)(4,1)S(1)} %broadcast_compare_fusion), kind=kOutput, calls=%fused_computation.43 | output fusion | flops 8389631 | bytes 6426624 | tf_op jit(solution)/shard_map/sub | solution.py:613
  30.3 0.0 copy-done
  30.3 0.1 reshape.110
  30.5 0.5 fusion.13
  31.0 0.0 copy-start.1
  31.0 5.7 %convolution_convert_fusion = bf16[128,4096]{1,0:T(8,128)(2,1)} fusion(bf16[128,1024]{0,1:T(8,128)(2,1)S(1)} %bitcast.29, bf16[1024,4096]{1,0:T(8,128)(2,1)} %param.17), kind=kOutput, calls=%fused_computation.1 | convolution fusion | flops 1074266112 | bytes 9699328 | tf_op jit(solution)/shard_map/dot_general | solution.py:626
  36.7 0.0 copy-done.1
  36.7 0.7 copy.22.ids_ref
  37.4 73.9 %shard_map.119 = (bf16[32,4096]{1,0:T(8,128)(2,1)}, bf16[4,128,1792]{2,1,0:T(8,128)(2,1)}, bf16[4,256,128]{2,1,0:T(8,128)(2,1)}, f32[4,256,128]{2,1,0:T(8,128)}) custom-call(bf16[2,2,32,4096]{3,2,1,0:T(8,128)(2,1)} %bitcast.27, bf16[32,4096]{1,0:T(8,128)(2,1)} %resid_ref.1, f32[1,4096]{1,0:T(1,128)} %bitcast.32, f32[4,4096]{1,0:T(4,128)} %bitcast.31, ...), custom_call_target="tpu_custom_call" | custom-call | tf_op jit(solution)/shard_map/pallas_call | solution.py:386
  111.3 64.3 %shard_map.120 = bf16[32,4096]{1,0:T(8,128)(2,1)} custom-call(bf16[4,128,1792]{2,1,0:T(8,128)(2,1)} %get-tuple-element.13.hidden_ref, bf16[4,256,128]{2,1,0:T(8,128)(2,1)} %get-tuple-element.14.placing_ref, f32[4,256,128]{2,1,0:T(8,128)} %get-tuple-element.15.weight_ref, bf16[1,1792,4096]{2,1,0:T(8,128)(2,1)} %down_ref.1, ...), custom_call_target="tpu_custom_call" | custom-call | tf_op jit(solution)/shard_map/pallas_call | solution.py:553
  175.6 1.7 copy.37
  (4 shorter events, 0.0 us)
Async XLA Ops:
  28.0 2.3 %copy-start = (bf16[8,128,256]{2,1,0:T(8,128)(2,1)S(1)}, bf16[8,128,256]{2,1,0:T(8,128)(2,1)}, u32[]{:S(2)}) copy-start(bf16[8,128,256]{2,1,0:T(8,128)(2,1)} %get-tuple-element.11) | copy-start | bytes 1572868
  31.0 5.7 %copy-start.1 = (s32[32,2]{0,1:T(2,128)S(1)}, s32[32,2]{0,1:T(2,128)}, u32[]{:S(2)}) copy-start(s32[32,2]{0,1:T(2,128)} %param.20) | copy-start | bytes 772
where the time goes:
time: 178 us; the launch traced here: 177 us
  Pallas kernels  162 us (91%)
  matrix products  6.9 us (4%)
  local copies, waits for them, and re-layouts  4.78 us (3%)
  other arithmetic  3.98 us (2%)
    pallas_call x1, Pallas kernels, stream_and_hidden(): pl.pallas_call(functools.partial(stream_kernel, levels, sub, model, model...  73.9 us
    pallas_call x1, Pallas kernels, sum_terms(): pl.pallas_call(functools.partial(sum_kernel, levels, sub, model, half, ti...  64.3 us
    pallas_call x1, Pallas kernels, gather_keys(): pl.pallas_call(functools.partial(gather_keys_kernel, levels), out_shape=(...  23.3 us
    dot_general x1, matrix products, on_device(): jnp.dot(attended, out_weight, preferred_element_type=jnp.float32)  5.67 us

commit v1 on v0

--- a/solution.py
+++ b/solution.py
@@ -126,6 +126,15 @@
 
 def at(z, x, y, c):
     return (z * 2 + x, y * 2 + c)
+
+
+def level_at(z, turn, levels):
+    upper = z // (levels // 2)
+    sign = 1 - 2 * upper
+    inner = z * (1 - upper) + (levels - 1 - z) * upper
+    beyond = jnp.minimum(jnp.maximum(turn - 2 * inner, 0), 1)
+    step = (turn + 1) // 2 * (1 if turn % 2 else -1)
+    return z + sign * ((1 - beyond) * step + beyond * (turn - inner))
 
 
 def greet(devices):
@@ -265,10 +274,29 @@
 
     left, right = slice(0, half), slice(half, model + 128)
     copies = [second] + first
-    own = out_ref.at[mine]
-    z_copies = [None] + [
-        start_send(own, own, zs.at[d], zr.at[d], z_peers[d - 1]) for d in range(1, levels)
-    ]
+    z_sides = ((1, z < levels - 1), (-1, z > 0))
+
+    def z_copy(side, k):
+        ref = out_ref.at[block(k, x, y)]
+        return pltpu.make_async_remote_copy(
+            src_ref=ref,
+            dst_ref=ref,
+            send_sem=zs.at[side, k],
+            recv_sem=zr.at[k],
+            device_id=at(z + z_sides[side][0], x, y, c),
+            device_id_type=MESH,
+        )
+
+    def z_pass(k, whole):
+        for side, (step, there) in enumerate(z_sides):
+            behind = (z - k) * step
+
+            @pl.when(jnp.logical_and(there, behind >= 0 if whole else behind > 0))
+            def _():
+                z_copy(side, k).start()
+
+    z_pass(z, True)
+    at_end = z % (levels - 1) == 0
     x_copies, y_copies, d_copies, e_copies, c_copies = [], [], [], [], []
 
     def to_core(index):
@@ -280,7 +308,7 @@
     sent = {d: [] for d in range(levels)}
 
     def finish(d):
-        k = (z + levels - d) % levels
+        k = level_at(z, d, levels)
         d_copies[d].wait_recv()
         e_copies[d].wait_recv()
         sent[d].append(to_core(block(k, 1 - x, 1 - y)))
@@ -289,7 +317,7 @@
     count = 8 * sub
 
     def experts_of(d):
-        k = (z + levels - d) % levels
+        k = level_at(z, d, levels)
         for n in sent[d]:
             c_copies[n].wait_recv()
         info = out_ref[pl.ds(k * 8, 8), :, model : model + 128].reshape(count, 128)
@@ -323,14 +351,14 @@
         picked_rows = jnp.where(at_slot == slot, 1.0, 0.0).T.astype(jnp.bfloat16)
 
         def pick(j, carry):
-            columns = pl.ds(pl.multiple_of(j * 512, 512), 512)
-            block_in = out_ref[pl.ds(k * 8, 8), :, columns].reshape(count, 512)
+            columns = pl.ds(pl.multiple_of(j * 1024, 1024), 1024)
+            block_in = out_ref[pl.ds(k * 8, 8), :, columns].reshape(count, 1024)
             rows_ref[:, columns] = jnp.dot(
                 picked_rows, block_in, preferred_element_type=jnp.float32
             ).astype(jnp.bfloat16)
             return carry
 
-        lax.fori_loop(0, model // 512, pick, 0)
+        lax.fori_loop(0, model // 1024, pick, 0)
         if d == 0:
             for load in loads:
                 load.wait()
@@ -347,16 +375,23 @@
 
     for turn in range(levels + 1):
         if turn < levels:
-            k = (z + levels - turn) % levels
-            if turn:
-                z_copies[turn].wait_recv()
+            k = level_at(z, turn, levels)
+            if 0 < turn < levels - 1:
+                z_copy(0, k).wait_recv()
+                z_pass(k, False)
+            elif turn:
+
+                @pl.when(at_end)
+                def _():
+                    z_copy(0, k).wait_recv()
+
             ref = out_ref.at[block(k, x, y)]
             x_copies.append(start_send(ref, ref, xs.at[turn], xr.at[turn], x_peer))
             y_copies.append(start_send(ref, ref, ys.at[turn], yr.at[turn], y_peer))
             sent[turn].append(to_core(block(k, x, y)))
         if turn:
             d = turn - 1
-            k = (z + levels - d) % levels
+            k = level_at(z, d, levels)
             x_copies[d].wait_recv()
             ref = out_ref.at[block(k, 1 - x, y), :, left]
             d_copies.append(start_send(ref, ref, ds.at[d], dr.at[d], y_peer))
@@ -367,11 +402,25 @@
             sent[d].append(to_core(block(k, x, 1 - y)))
         if turn >= 2:
             finish(turn - 2)
+            if turn == levels - 2:
+                k = level_at(z, levels - 1, levels)
+
+                @pl.when(jnp.logical_not(at_end))
+                def _():
+                    z_copy(0, k).wait_recv()
+                    z_pass(k, False)
+
             experts_of(turn - 2)
     finish(levels - 1)
     experts_of(levels - 1)
-    for copy in copies + z_copies[1:] + x_copies + y_copies + d_copies + e_copies + c_copies:
+    for copy in copies + x_copies + y_copies + d_copies + e_copies + c_copies:
         copy.wait_send()
+    for k in range(levels):
+        for side, (step, there) in enumerate(z_sides):
+
+            @pl.when(jnp.logical_and(there, (z - k) * step >= 0))
+            def _():
+                z_copy(side, k).wait_send()
 
 
 def stream_and_hidden(projected, resid_in, norm_gain, router, expert_ids, gate, up, levels):
@@ -385,7 +434,7 @@
     bf16 = jnp.bfloat16
     return pl.pallas_call(
         functools.partial(
-            stream_kernel, levels, sub, model, model // 2, experts, slots, width // 7
+            stream_kernel, levels, sub, model, model // 2, experts, slots, width // 2
         ),
         out_shape=(
             jax.ShapeDtypeStruct((sub, model), bf16),
@@ -406,7 +455,8 @@
             dma((3,)),
             dma((3,)),
         ]
-        + [dma((levels,))] * 10
+        + [dma((2, levels))]
+        + [dma((levels,))] * 9
         + [dma((levels * 4,))] * 2
         + [dma((model // LOAD_ROWS,))] * 2,
         compiler_params=pltpu.CompilerParams(
@@ -425,7 +475,7 @@
 
 def sum_kernel(
     levels, sub, model, half, tile, hidden_ref, placing_ref, weight_ref, down_ref, stream_ref,
-    out_ref, part_ref, down_w, core_in, held, a_in, b_in, a2_in, b2_in, ready, z_in,
+    out_ref, part_ref, down_w, core_in, held, a_in, b_in, a2_in, b2_in, ready, z_in, total,
     cs, cr, sa, ra, sb, rb, sa2, ra2, sb2, rb2, zs, zr, ls,
 ):
     loads = []
@@ -439,13 +489,16 @@
     x_peer, y_peer, c_peer = at(z, 1 - x, y, c), at(z, x, 1 - y, c), at(z, x, y, 1 - c)
     z_peers = [at((z + d) % levels, x, y, c) for d in range(1, levels)]
     greet(z_peers + [x_peer, y_peer, c_peer])
-    turns = list(range(1, levels)) + [0]
+    turns = list(range(levels))
     left, right = slice(0, half), slice(half, model)
     f32, bf16 = jnp.float32, jnp.bfloat16
     c_copies = [None] * levels
 
+    def target(d):
+        return level_at(z, levels - 1 - d, levels)
+
     def terms_of(d):
-        k = (z + d) % levels
+        k = target(d)
         lanes = weight_ref[k]
         weight = jnp.concatenate([lanes] * (tile // 128), axis=1)
         hidden = hidden_ref[k]
@@ -473,11 +526,38 @@
             part_ref.at[k, :, :, 1 - c], core_in.at[d], cs.at[d], cr.at[d], c_peer
         )
     terms_of(turns[0])
-    stage2, stage3, z_copies = {}, {}, {}
+    stage2, stage3 = {}, {}
+    z_sides = ((1, z > 0), (-1, z < levels - 1))
+
+    def z_copy(d, side):
+        k = target(d)
+        return pltpu.make_async_remote_copy(
+            src_ref=ready.at[d],
+            dst_ref=z_in.at[side, k],
+            send_sem=zs.at[d],
+            recv_sem=zr.at[side, k],
+            device_id=at(z + z_sides[side][0], x, y, c),
+            device_id_type=MESH,
+        )
+
+    def z_send(d, with_outer):
+        ahead = target(d) - z
+        for side, (step, outer) in enumerate(z_sides):
+            right_way = ahead * step > 0
+
+            @pl.when(jnp.logical_and(right_way, outer if with_outer else jnp.logical_not(outer)))
+            def _():
+                if with_outer:
+                    z_copy(d, side).wait_recv()
+                    ready[d] = (
+                        ready[d].astype(f32) + z_in[side, target(d)].astype(f32)
+                    ).astype(bf16)
+                z_copy(d, side).start()
+
     for step in range(levels + 2):
         if step < levels:
             d = turns[step]
-            k = (z + d) % levels
+            k = target(d)
             c_copies[d].wait_recv()
             for bx in range(2):
                 for by in range(2):
@@ -522,31 +602,36 @@
                 + b_in[d, y].astype(f32)
                 + b2_in[d].astype(f32)
             )
-            if d:
+            if d < levels - 1:
                 ready[d, :, left] = low.astype(bf16)
                 ready[d, :, right] = high.astype(bf16)
-                z_copies[d] = start_send(
-                    ready.at[d], z_in.at[d], zs.at[d], zr.at[d], z_peers[d - 1]
-                )
+                z_send(d, False)
             else:
-                for d in range(1, levels):
-                    z_copies[d].wait_recv()
-                    low = low + z_in[d, :, left].astype(f32)
-                    high = high + z_in[d, :, right].astype(f32)
-                out_ref[:, left] = (stream_ref[:, left].astype(f32) + low).astype(bf16)
-                out_ref[:, right] = (stream_ref[:, right].astype(f32) + high).astype(bf16)
+                total[:, left] = stream_ref[:, left].astype(f32) + low
+                total[:, right] = stream_ref[:, right].astype(f32) + high
+        for d in range(levels - 1):
+            if step == (d + 3 if d < levels - 2 else d + 2):
+                z_send(d, True)
+    for side, (_, outer) in enumerate(z_sides):
+
+        @pl.when(outer)
+        def _():
+            z_copy(levels - 1, side).wait_recv()
+            total[...] += z_in[side, z].astype(f32)
+
+    out_ref[...] = total[...].astype(bf16)
     for d in range(levels):
         c_copies[d].wait_send()
         for copy in stage2[d]:
             copy.wait_send()
-        if d:
-            z_copies[d].wait_send()
+        if d < levels - 1:
+            z_copy(d, 0).wait_send()
 
 
 def sum_terms(hidden, placing, weight, down, stream, levels):
     sub, model = stream.shape
     half = model // 2
-    tile = 512
+    tile = 1024
     vmem = pl.BlockSpec(memory_space=pltpu.VMEM)
     dma = pltpu.SemaphoreType.DMA
     bf16 = jnp.bfloat16
@@ -565,9 +650,11 @@
             pltpu.VMEM((levels, sub, half), bf16),
             pltpu.VMEM((levels, sub, half), bf16),
             pltpu.VMEM((levels, sub, model), bf16),
-            pltpu.VMEM((levels, sub, model), bf16),
+            pltpu.VMEM((2, levels, sub, model), bf16),
+            pltpu.VMEM((sub, model), jnp.float32),
         ]
-        + [dma((levels,))] * 12
+        + [dma((levels,))] * 11
+        + [dma((2, levels))]
         + [dma((model // tile,))],
         compiler_params=pltpu.CompilerParams(
             collective_id=2, has_side_effects=True, vmem_limit_bytes=VMEM_BYTES
@@ -651,7 +738,7 @@
 
     def body(queries, keys, values, resid_in, *rest):
         blocks = resid_in.size * mesh.size * 2
-        small = mesh.shape["exp"] == 4 and mesh.shape["ctx"] % 2 == 0 and blocks * 4 <= VMEM_BYTES
+        small = mesh.shape["exp"] == 4 and levels == 4 and blocks * 4 <= VMEM_BYTES
         local = functools.partial(on_device, levels) if small else on_device_xla
         return local(queries, keys, values, resid_in, *rest)
 

time: 178 us -> 160 us (0.90)
  Pallas kernels: 162 us -> 144 us
    pallas_call x1, Pallas kernels: 64.3 us -> 52.2 us  [sum_terms(): pl.pallas_call(functools.partial(sum_kernel, levels, sub, model, half, ti...]
    pallas_call x1, Pallas kernels: 73.9 us -> 68.2 us  [stream_and_hidden(): pl.pallas_call(functools.partial(stream_kernel, levels, sub, model, model...]
where the time goes in v1:
time: 160 us; the launch traced here: 159 us
  Pallas kernels  144 us (90%)
  matrix products  6.9 us (4%)
  local copies, waits for them, and re-layouts  4.78 us (3%)
  other arithmetic  3.98 us (2%)
    pallas_call x1, Pallas kernels, stream_and_hidden(): pl.pallas_call(functools.partial(stream_kernel, levels, sub, model, model...  68.2 us
    pallas_call x1, Pallas kernels, sum_terms(): pl.pallas_call(functools.partial(sum_kernel, levels, sub, model, half, ti...  52.2 us
    pallas_call x1, Pallas kernels, gather_keys(): pl.pallas_call(functools.partial(gather_keys_kernel, levels), out_shape=(...  23.3 us
    dot_general x1, matrix products, on_device(): jnp.dot(attended, out_weight, preferred_element_type=jnp.float32)  5.67 us

profile of v1, /device:TPU:0, one launch (start us, length us, event | category | flops | bytes accessed | tf_op | source)
XLA Modules:
  0.0 159.5 jit_solution(1645588627486764977)
XLA Ops:
  0.0 0.7 select_reduce_fusion.1
  0.8 0.7 select_reduce_fusion
  1.5 0.2 broadcast_compare_fusion
  1.7 23.3 %shard_map.118 = (bf16[8,128,256]{2,1,0:T(8,128)(2,1)}, bf16[8,128,256]{2,1,0:T(8,128)(2,1)}) custom-call(bf16[128,256]{1,0:T(8,128)(2,1)} %k_ref.1, bf16[128,256]{1,0:T(8,128)(2,1)} %v_ref.1), custom_call_target="tpu_custom_call" | custom-call | tf_op jit(solution)/shard_map/pallas_call | solution.py:193
  25.0 1.2 reshape.111
  26.2 1.1 reshape.112
  27.3 0.7 fusion.16
  28.0 0.0 copy-start
  28.1 2.3 %fusion.31 = (f32[2,4,128]{2,1,0:T(4,128)S(1)}, bf16[2,4,128,1024]{2,3,1,0:T(8,128)(2,1)S(1)}) fusion(f32[2,1024,128,4]{2,1,3,0:T(8,128)S(1)} %fusion.16, pred[128,1024]{0,1:T(8,128)(4,1)S(1)} %broadcast_compare_fusion), kind=kOutput, calls=%fused_computation.43 | output fusion | flops 8389631 | bytes 6426624 | tf_op jit(solution)/shard_map/sub | solution.py:700
  30.3 0.0 copy-done
  30.3 0.1 reshape.110
  30.5 0.5 fusion.13
  31.0 0.0 copy-start.1
  31.0 5.7 %convolution_convert_fusion = bf16[128,4096]{1,0:T(8,128)(2,1)} fusion(bf16[128,1024]{0,1:T(8,128)(2,1)S(1)} %bitcast.29, bf16[1024,4096]{1,0:T(8,128)(2,1)} %param.17), kind=kOutput, calls=%fused_computation.1 | convolution fusion | flops 1074266112 | bytes 9699328 | tf_op jit(solution)/shard_map/dot_general | solution.py:713
  36.7 0.0 copy-done.1
  36.7 0.7 copy.22.ids_ref
  37.4 68.2 %shard_map.119 = (bf16[32,4096]{1,0:T(8,128)(2,1)}, bf16[4,128,1792]{2,1,0:T(8,128)(2,1)}, bf16[4,256,128]{2,1,0:T(8,128)(2,1)}, f32[4,256,128]{2,1,0:T(8,128)}) custom-call(bf16[2,2,32,4096]{3,2,1,0:T(8,128)(2,1)} %bitcast.27, bf16[32,4096]{1,0:T(8,128)(2,1)} %resid_ref.1, f32[1,4096]{1,0:T(1,128)} %bitcast.32, f32[4,4096]{1,0:T(4,128)} %bitcast.31, ...), custom_call_target="tpu_custom_call" | custom-call | tf_op jit(solution)/shard_map/pallas_call | solution.py:435
  105.6 52.2 %shard_map.120 = bf16[32,4096]{1,0:T(8,128)(2,1)} custom-call(bf16[4,128,1792]{2,1,0:T(8,128)(2,1)} %get-tuple-element.13.hidden_ref, bf16[4,256,128]{2,1,0:T(8,128)(2,1)} %get-tuple-element.14.placing_ref, f32[4,256,128]{2,1,0:T(8,128)} %get-tuple-element.15.weight_ref, bf16[1,1792,4096]{2,1,0:T(8,128)(2,1)} %down_ref.1, ...), custom_call_target="tpu_custom_call" | custom-call | tf_op jit(solution)/shard_map/pallas_call | solution.py:638
  157.8 1.7 %copy.37 = bf16[32,4096]{1,0:T(8,128)(2,1)} copy(bf16[32,4096]{1,0:T(8,128)(2,1)} %shard_map.120) | data formatting | bytes 524288
  (4 shorter events, 0.0 us)
Async XLA Ops:
  28.0 2.3 %copy-start = (bf16[8,128,256]{2,1,0:T(8,128)(2,1)S(1)}, bf16[8,128,256]{2,1,0:T(8,128)(2,1)}, u32[]{:S(2)}) copy-start(bf16[8,128,256]{2,1,0:T(8,128)(2,1)} %get-tuple-element.11) | copy-start | bytes 1572868
  31.0 5.7 %copy-start.1 = (s32[32,2]{0,1:T(2,128)S(1)}, s32[32,2]{0,1:T(2,128)}, u32[]{:S(2)}) copy-start(s32[32,2]{0,1:T(2,128)} %param.20) | copy-start | bytes 772

commit v2 on v1

v2 whole, which is shorter than its diff:
```python
import functools
import math

import jax
import jax.numpy as jnp
from jax import lax
from jax.experimental import pallas as pl
from jax.experimental.pallas import tpu as pltpu
from jax.sharding import PartitionSpec as P

HEAD_SIZE = 128
SPAN = 64


def true_positions(row_ids, span_order):
    span_ids = jnp.arange(span_order.shape[0], dtype=jnp.int32)
    matches = (row_ids // SPAN)[:, None] == span_ids[None, :]
    return jnp.sum(jnp.where(matches, span_order[None, :], 0), axis=1) * SPAN + row_ids % SPAN


def on_device_xla(
    queries,
    keys,
    values,
    resid_in,
    span_order,
    out_weight,
    norm_gain,
    router,
    expert_ids,
    w_gate,
    w_up,
    w_down,
):
    tok_rows = queries.shape[0]
    kv_heads = keys.shape[1] // HEAD_SIZE
    head_cluster = queries.shape[1] // HEAD_SIZE // kv_heads
    ctx_index = lax.axis_index("ctx")
    query_pos = true_positions(
        ctx_index * tok_rows + jnp.arange(tok_rows, dtype=jnp.int32), span_order
    )
    shaped_queries = queries.reshape(tok_rows, kv_heads, head_cluster, HEAD_SIZE)
    score_scale = 1.0 / math.sqrt(HEAD_SIZE)
    pieces = (
        lax.all_gather(keys, "ctx", axis=0, tiled=True),
        lax.all_gather(values, "ctx", axis=0, tiled=True),
    )
    key_pos = true_positions(jnp.arange(pieces[0].shape[0], dtype=jnp.int32), span_order)
    running_max = jnp.full((kv_heads, head_cluster, tok_rows), -1e30, jnp.float32)
    key_block, value_block = pieces
    key_count = key_block.shape[0]
    key_head_rows = key_block.reshape(key_count, kv_heads, HEAD_SIZE)
    value_head_rows = value_block.reshape(key_count, kv_heads, HEAD_SIZE)
    scores = jnp.einsum(
        "qhgd,khd->hgqk", shaped_queries, key_head_rows, preferred_element_type=jnp.float32
    )
    allowed = key_pos[None, :] <= query_pos[:, None]
    scores = jnp.where(allowed[None, None], scores * score_scale, -1e30)
    new_max = jnp.maximum(running_max, jnp.max(scores, axis=-1))
    weights = jnp.where(allowed[None, None], jnp.exp(scores - new_max[..., None]), 0.0)
    running_sum = jnp.sum(weights, axis=-1)
    update = jnp.einsum(
        "hgqk,khd->qhgd",
        weights.astype(jnp.bfloat16),
        value_head_rows,
        preferred_element_type=jnp.float32,
    )
    weighted = update
    running_max, running_sum, weighted = (new_max, running_sum, weighted)
    attended = (
        (weighted / jnp.transpose(running_sum, (2, 0, 1))[..., None])
        .astype(jnp.bfloat16)
        .reshape(tok_rows, -1)
    )
    projected = jnp.dot(attended, out_weight, preferred_element_type=jnp.float32)
    own_sum = lax.psum_scatter(
        projected.astype(jnp.bfloat16), "exp", scatter_dimension=0, tiled=True
    ).astype(jnp.float32)
    stream = (resid_in.astype(jnp.float32) + own_sum).astype(jnp.bfloat16)
    stream_wide = stream.astype(jnp.float32)
    mean_square = jnp.mean(stream_wide * stream_wide, axis=-1, keepdims=True)
    normed = (stream_wide * lax.rsqrt(mean_square + 1e-05) * norm_gain).astype(jnp.bfloat16)
    model_dim = normed.shape[1]
    logits = jnp.dot(normed.astype(jnp.float32), router, precision=lax.Precision.HIGHEST)
    experts = router.shape[1]
    expert_axis = jnp.arange(experts, dtype=jnp.int32)
    picked = expert_ids[:, :, None] == expert_axis[None, None, :]
    chosen = jnp.sum(jnp.where(picked, logits[:, None, :], 0.0), axis=-1)
    mixing = jax.nn.softmax(chosen, axis=-1)
    token_weight = jnp.sum(jnp.where(picked, mixing[:, :, None], 0.0), axis=1)
    routed = jnp.any(picked, axis=1)
    rank_of = jnp.cumsum(routed.astype(jnp.int32), axis=0) - 1
    slot_count = resid_in.shape[0] * expert_ids.shape[1] // experts
    slot_axis = jnp.arange(slot_count, dtype=jnp.int32)
    placing = jnp.logical_and(
        routed.T[:, None, :], rank_of.T[:, None, :] == slot_axis[None, :, None]
    )
    outgoing = jnp.einsum(
        "est,td->esd", placing.astype(jnp.bfloat16), normed, preferred_element_type=jnp.float32
    ).astype(jnp.bfloat16)
    arrived = lax.all_to_all(outgoing, "exp", split_axis=0, concat_axis=0, tiled=True)
    rows_in = lax.all_gather(arrived.reshape(-1, model_dim), "ctx", axis=0, tiled=True)
    gate_part = jnp.dot(rows_in, w_gate[0], preferred_element_type=jnp.float32)
    up_part = jnp.dot(rows_in, w_up[0], preferred_element_type=jnp.float32)
    hidden = (jax.nn.silu(gate_part) * up_part).astype(jnp.bfloat16)
    partials = jnp.dot(hidden, w_down[0], preferred_element_type=jnp.float32)
    own_rows = lax.psum_scatter(
        partials.astype(jnp.bfloat16), "ctx", scatter_dimension=0, tiled=True
    )
    results = own_rows.reshape(experts, slot_count, model_dim)
    returned = lax.all_to_all(results, "exp", split_axis=0, concat_axis=0, tiled=True)
    coefficient = placing.astype(jnp.float32) * token_weight.T[:, None, :]
    combined = jnp.einsum("est,esd->td", coefficient, returned.astype(jnp.float32))
    return (stream_wide + combined).astype(jnp.bfloat16)


VMEM_BYTES = 60 * 2**20
LOAD_ROWS = 512
MESH = pl.DeviceIdType.MESH


def place_of():
    ctx, exp = lax.axis_index("ctx"), lax.axis_index("exp")
    return ctx // 2, ctx % 2, exp // 2, exp % 2


def at(z, x, y, c):
    return (z * 2 + x, y * 2 + c)


def level_at(z, turn, levels):
    upper = z // (levels // 2)
    sign = 1 - 2 * upper
    inner = z * (1 - upper) + (levels - 1 - z) * upper
    beyond = jnp.minimum(jnp.maximum(turn - 2 * inner, 0), 1)
    step = (turn + 1) // 2 * (1 if turn % 2 else -1)
    return z + sign * ((1 - beyond) * step + beyond * (turn - inner))


def neighbours(z, x, y, c, levels):
    return (
        (at(z, 1 - x, y, c), None),
        (at(z, x, 1 - y, c), None),
        (at(z, x, y, 1 - c), None),
        (at(z - 1, x, y, c), z > 0),
        (at(z + 1, x, y, c), z < levels - 1),
    )


def announce(z, x, y, c, levels):
    barrier = pltpu.get_barrier_semaphore()
    for device, there in neighbours(z, x, y, c, levels):

        def signal():
            pl.semaphore_signal(barrier, inc=1, device_id=device, device_id_type=MESH)

        if there is None:
            signal()
        else:
            pl.when(there)(signal)


def meet(z, levels):
    beside = jnp.minimum(z, 1) + jnp.minimum(levels - 1 - z, 1)
    pl.semaphore_wait(pltpu.get_barrier_semaphore(), 3 + beside)


def start_send(src, dst, send_sem, recv_sem, device):
    copy = pltpu.make_async_remote_copy(
        src_ref=src,
        dst_ref=dst,
        send_sem=send_sem,
        recv_sem=recv_sem,
        device_id=device,
        device_id_type=MESH,
    )
    copy.start()
    return copy


def attend_kernel(
    levels, heads, group, parts, q_ref, k_ref, v_ref, pos_ref, resid_ref, weight_ref, stream_ref,
    weight, k_in, v_in, stacked, top, total, mixed, attended, projected, core_in, kept, from_y,
    ws, zs, zr, xs, xr, cs, cr, ys, yr,
):
    f32, bf16 = jnp.float32, jnp.bfloat16
    rows_per_load = weight.shape[0] // parts
    loads = []
    for part in range(parts):
        rows = slice(part * rows_per_load, (part + 1) * rows_per_load)
        loads.append(pltpu.make_async_copy(weight_ref.at[rows], weight.at[rows], ws.at[part]))
        loads[part].start()
    z, x, y, c = place_of()
    x_peer, y_peer, c_peer = at(z, 1 - x, y, c), at(z, x, 1 - y, c), at(z, x, y, 1 - c)
    announce(z, x, y, c, levels)
    meet(z, levels)
    own, incoming = (k_ref, v_ref), (k_in, v_in)
    z_sides = ((1, z < levels - 1), (-1, z > 0))
    mine = z * 2 + x

    def z_copy(i, side, k, first=False):
        ref = incoming[i].at[k * 2 + x]
        return pltpu.make_async_remote_copy(
            src_ref=own[i] if first else ref,
            dst_ref=ref,
            send_sem=zs.at[i, side, k],
            recv_sem=zr.at[i, k],
            device_id=at(z + z_sides[side][0], x, y, c),
            device_id_type=MESH,
        )

    def x_copy(i, k, first=False):
        ref = incoming[i].at[k * 2 + x]
        return pltpu.make_async_remote_copy(
            src_ref=own[i] if first else ref,
            dst_ref=ref,
            send_sem=xs.at[i, k],
            recv_sem=xr.at[i, k],
            device_id=x_peer,
            device_id_type=MESH,
        )

    def from_peer(i, k):
        ref = incoming[i].at[k * 2 + 1 - x]
        return pltpu.make_async_remote_copy(
            src_ref=ref,
            dst_ref=ref,
            send_sem=xs.at[i, k],
            recv_sem=xr.at[i, k],
            device_id=x_peer,
            device_id_type=MESH,
        )

    for i in range(2):
        for side, (_, there) in enumerate(z_sides):

            @pl.when(there)
            def _():
                z_copy(i, side, z, True).start()

        x_copy(i, z, True).start()

    rows = q_ref.shape[0]
    size = q_ref.shape[1] // (heads * group)
    for h in range(heads):
        for g in range(group):
            head = h * group + g
            stacked[h, g * rows : (g + 1) * rows, :] = q_ref[:, head * size : (head + 1) * size]
    query_pos = jnp.broadcast_to(pos_ref[mine], (rows, rows)).T
    scale = 1.0 / math.sqrt(size)

    def attend(keys, values, index, first=False):
        allowed = (pos_ref[index] <= query_pos)[None]

        def one(h, carry):
            columns = pl.ds(pl.multiple_of(h * size, size), size)
            scores = lax.dot_general(
                stacked[h], keys[:, columns], (((1,), (1,)), ((), ())), preferred_element_type=f32
            ).reshape(group, rows, rows)
            scores = jnp.where(allowed, scores * scale, -1e30)
            new_top = jnp.max(scores, axis=-1, keepdims=True)
            if not first:
                new_top = jnp.maximum(top[h], new_top)
            weights = jnp.where(allowed, jnp.exp(scores - new_top), 0.0)
            new_total = jnp.sum(weights, axis=-1, keepdims=True)
            update = jnp.dot(
                weights.astype(bf16).reshape(group * rows, rows),
                values[:, columns],
                preferred_element_type=f32,
            ).reshape(group, rows, size)
            if not first:
                fade = jnp.exp(top[h] - new_top)
                new_total = new_total + fade * total[h]
                update = update + fade * mixed[h]
            top[h] = new_top
            total[h] = new_total
            mixed[h] = update
            return carry

        lax.fori_loop(0, heads, one, 0)

    attend(k_ref, v_ref, mine, True)
    for turn in range(1, levels + 1):
        if turn < levels:
            k = level_at(z, turn, levels)
            for i in range(2):
                z_copy(i, 0, k).wait_recv()
                for side, (step, there) in enumerate(z_sides):

                    @pl.when(jnp.logical_and(there, (z - k) * step > 0))
                    def _():
                        z_copy(i, side, k).start()

                x_copy(i, k).start()
        last = level_at(z, turn - 1, levels)
        for i in range(2):
            from_peer(i, last).wait_recv()
        index = last * 2 + 1 - x
        attend(k_in.at[index], v_in.at[index], index)
        if turn < levels:
            attend(k_in.at[k * 2 + x], v_in.at[k * 2 + x], k * 2 + x)

    for h in range(heads):
        result = (mixed[h] / total[h]).astype(bf16)
        for g in range(group):
            head = h * group + g
            attended[:, head * size : (head + 1) * size] = result[g]
    for load in loads:
        load.wait()

    width = weight.shape[1] // parts
    sub = resid_ref.shape[0]
    c_copies, y_copies = [], []

    def cut(part):
        return slice(part * width, (part + 1) * width)

    def pass_on(part):
        c_copies[part].wait_recv()
        kept[part] = (
            projected[part, 1 - y, c].astype(f32) + core_in[part, 1 - y].astype(f32)
        ).astype(bf16)
        y_copies.append(
            start_send(kept.at[part], from_y.at[part], ys.at[part], yr.at[part], y_peer)
        )

    for part in range(parts):
        projected[part] = (
            jnp.dot(attended[...], weight[:, cut(part)], preferred_element_type=f32)
            .astype(bf16)
            .reshape(2, 2, sub, width)
        )
        c_copies.append(
            start_send(
                projected.at[part, :, 1 - c], core_in.at[part], cs.at[part], cr.at[part], c_peer
            )
        )
        if part:
            pass_on(part - 1)
    pass_on(parts - 1)
    for part in range(parts):
        own_sum = projected[part, y, c].astype(f32) + core_in[part, y].astype(f32)
        own_sum = own_sum + resid_ref[:, cut(part)].astype(f32)
        y_copies[part].wait_recv()
        stream_ref[:, cut(part)] = (own_sum + from_y[part].astype(f32)).astype(bf16)
    for copy in c_copies + y_copies:
        copy.wait_send()
    for i in range(2):
        for k in range(levels):
            x_copy(i, k).wait_send()
            for side, (step, there) in enumerate(z_sides):

                @pl.when(jnp.logical_and(there, (z - k) * step >= 0))
                def _():
                    z_copy(i, side, k).wait_send()


def attend(queries, keys, values, positions, resid_in, out_weight, levels):
    rows, width = keys.shape
    sub, model = resid_in.shape
    heads = width // HEAD_SIZE
    group = queries.shape[1] // width
    parts = 4
    vmem = pl.BlockSpec(memory_space=pltpu.VMEM)
    dma = pltpu.SemaphoreType.DMA
    f32, bf16 = jnp.float32, jnp.bfloat16
    return pl.pallas_call(
        functools.partial(attend_kernel, levels, heads, group, parts),
        out_shape=jax.ShapeDtypeStruct((sub, model), bf16),
        in_specs=[vmem] * 5 + [pl.BlockSpec(memory_space=pl.ANY)],
        out_specs=vmem,
        scratch_shapes=[
            pltpu.VMEM(out_weight.shape, bf16),
            pltpu.VMEM((levels * 2, rows, width), bf16),
            pltpu.VMEM((levels * 2, rows, width), bf16),
            pltpu.VMEM((heads, group * rows, HEAD_SIZE), bf16),
            pltpu.VMEM((heads, group, rows, 1), f32),
            pltpu.VMEM((heads, group, rows, 1), f32),
            pltpu.VMEM((heads, group, rows, HEAD_SIZE), f32),
            pltpu.VMEM(queries.shape, bf16),
            pltpu.VMEM((parts, 2, 2, sub, model // parts), bf16),
            pltpu.VMEM((parts, 2, sub, model // parts), bf16),
            pltpu.VMEM((parts, sub, model // parts), bf16),
            pltpu.VMEM((parts, sub, model // parts), bf16),
            dma((parts,)),
            dma((2, 2, levels)),
            dma((2, levels)),
            dma((2, levels)),
            dma((2, levels)),
        ]
        + [dma((parts,))] * 4,
        compiler_params=pltpu.CompilerParams(
            collective_id=0, has_side_effects=True, vmem_limit_bytes=VMEM_BYTES
        ),
    )(queries, keys, values, positions, resid_in, out_weight)


def stream_kernel(
    levels, sub, model, half, experts, slots, tile, stream_ref, gain_ref, router_ref,
    ids_ref, gate_ref, up_ref, hidden_ref, placing_ref, weight_ref,
    out_ref, gate_w, up_w, rows_ref, zs, zr, xs, xr, ys, yr, ds, dr, es, er, cs, cr, gs, us,
):
    loads = []
    for part in range(model // LOAD_ROWS):
        rows = slice(part * LOAD_ROWS, (part + 1) * LOAD_ROWS)
        loads.append(pltpu.make_async_copy(gate_ref.at[0, rows], gate_w.at[rows], gs.at[part]))
        loads.append(pltpu.make_async_copy(up_ref.at[0, rows], up_w.at[rows], us.at[part]))
    for load in loads:
        load.start()
    z, x, y, c = place_of()
    x_peer, y_peer, c_peer = at(z, 1 - x, y, c), at(z, x, 1 - y, c), at(z, x, y, 1 - c)
    announce(z, x, y, c, levels)

    stream = stream_ref[...]
    wide = stream.astype(jnp.float32)
    mean_square = jnp.mean(wide * wide, axis=-1, keepdims=True)
    normed = (wide * lax.rsqrt(mean_square + 1e-05) * gain_ref[...]).astype(jnp.bfloat16)

    normed_wide = normed.astype(jnp.float32)
    logits = [
        jnp.sum(normed_wide * router_ref[e : e + 1, :], axis=-1, keepdims=True)
        for e in range(experts)
    ]
    token = lax.broadcasted_iota(jnp.int32, (sub, sub), 0)
    same = token == lax.broadcasted_iota(jnp.int32, (sub, sub), 1)
    id0, id1 = (
        jnp.sum(
            jnp.where(same, ids_ref[i : i + 1, :].astype(jnp.float32), 0.0), axis=1, keepdims=True
        ).astype(jnp.int32)
        for i in range(2)
    )
    zero = jnp.zeros_like(logits[0])
    pick0, pick1 = zero, zero
    for e in range(experts):
        pick0 = pick0 + jnp.where(id0 == e, logits[e], 0.0)
        pick1 = pick1 + jnp.where(id1 == e, logits[e], 0.0)
    top = jnp.maximum(pick0, pick1)
    exp0, exp1 = jnp.exp(pick0 - top), jnp.exp(pick1 - top)
    gate0, gate1 = exp0 / (exp0 + exp1), exp1 / (exp0 + exp1)
    lane = lax.broadcasted_iota(jnp.int32, (sub, 128), 1)
    expert = lane % experts
    routed = jnp.logical_or(expert == id0, expert == id1)
    weight = jnp.where(expert == id0, gate0, 0.0) + jnp.where(expert == id1, gate1, 0.0)
    high = weight.astype(jnp.bfloat16).astype(jnp.float32)
    group = lane // experts
    tail = jnp.where(
        group == 0,
        jnp.where(routed, 1.0, 0.0),
        jnp.where(group == 1, high, jnp.where(group == 2, weight - high, 0.0)),
    )

    def block(k, bx, by):
        return ((k * 2 + bx) * 2 + by) * 2 + c

    mine = block(z, x, y)
    out_ref[mine, :, 0:model] = normed
    out_ref[mine, :, model : model + 128] = tail.astype(jnp.bfloat16)

    left, right = slice(0, half), slice(half, model + 128)
    pieces = (left, right)
    z_sides = ((1, z < levels - 1), (-1, z > 0))

    def z_copy(side, k, p):
        ref = out_ref.at[block(k, x, y), :, pieces[p]]
        return pltpu.make_async_remote_copy(
            src_ref=ref,
            dst_ref=ref,
            send_sem=zs.at[side, p, k],
            recv_sem=zr.at[p, k],
            device_id=at(z + z_sides[side][0], x, y, c),
            device_id_type=MESH,
        )

    def z_pass(k, p, whole=False):
        for side, (step, there) in enumerate(z_sides):
            behind = (z - k) * step

            @pl.when(jnp.logical_and(there, behind >= 0 if whole else behind > 0))
            def _():
                z_copy(side, k, p).start()

    meet(z, levels)
    for p in range(2):
        z_pass(z, p, True)
    at_end = z % (levels - 1) == 0
    x_copies, y_copies, d_copies, e_copies, c_copies = [], [], [], [], []

    def to_core(index):
        n = len(c_copies)
        ref = out_ref.at[index]
        c_copies.append(start_send(ref, ref, cs.at[n], cr.at[n], c_peer))
        return n

    sent = {d: [] for d in range(levels)}

    def finish(d):
        k = level_at(z, d, levels)
        d_copies[d].wait_recv()
        e_copies[d].wait_recv()
        sent[d].append(to_core(block(k, 1 - x, 1 - y)))

    mine_expert = lax.axis_index("exp")
    count = 8 * sub

    def experts_of(d):
        k = level_at(z, d, levels)
        for n in sent[d]:
            c_copies[n].wait_recv()
        info = out_ref[pl.ds(k * 8, 8), :, model : model + 128].reshape(count, 128)
        above = lax.broadcasted_iota(jnp.int32, (count, count), 0)
        below = lax.broadcasted_iota(jnp.int32, (count, count), 1)
        within = jnp.logical_and(above // sub == below // sub, below <= above)
        seen = jnp.dot(
            jnp.where(within, 1.0, 0.0).astype(jnp.bfloat16),
            info,
            preferred_element_type=jnp.float32,
        )
        wide_info = info.astype(jnp.float32)
        at_lane = lax.broadcasted_iota(jnp.int32, (count, 128), 1)

        def lane_sum(value, keep):
            return jnp.sum(jnp.where(keep, value, 0.0), axis=1, keepdims=True)

        is_mine = at_lane == mine_expert
        here = lane_sum(wide_info, is_mine)
        rank = lane_sum(seen, is_mine).astype(jnp.int32) - 1
        token_weight = lane_sum(
            wide_info,
            jnp.logical_or(at_lane == experts + mine_expert, at_lane == 2 * experts + mine_expert),
        )
        token = lax.broadcasted_iota(jnp.int32, (count, 1), 0)
        slot = jnp.where(here > 0.5, token // sub * slots + rank, -1)
        at_slot = lax.broadcasted_iota(jnp.int32, (count, 8 * slots), 1)
        placing = jnp.where(at_slot == slot, 1.0, 0.0).astype(jnp.bfloat16)
        placing_ref[k] = placing
        weight_ref[k] = jnp.broadcast_to(token_weight, (count, 128))
        picked_rows = jnp.where(at_slot == slot, 1.0, 0.0).T.astype(jnp.bfloat16)

        def pick(j, carry):
            columns = pl.ds(pl.multiple_of(j * 1024, 1024), 1024)
            block_in = out_ref[pl.ds(k * 8, 8), :, columns].reshape(count, 1024)
            rows_ref[:, columns] = jnp.dot(
                picked_rows, block_in, preferred_element_type=jnp.float32
            ).astype(jnp.bfloat16)
            return carry

        lax.fori_loop(0, model // 1024, pick, 0)
        if d == 0:
            for load in loads:
                load.wait()

        def unit(j, carry):
            columns = pl.ds(pl.multiple_of(j * tile, tile), tile)
            rows = rows_ref[...]
            gate = jnp.dot(rows, gate_w[:, columns], preferred_element_type=jnp.float32)
            up = jnp.dot(rows, up_w[:, columns], preferred_element_type=jnp.float32)
            hidden_ref[k, :, columns] = (gate * jax.nn.sigmoid(gate) * up).astype(jnp.bfloat16)
            return carry

        lax.fori_loop(0, hidden_ref.shape[2] // tile, unit, 0)

    for turn in range(levels + 1):
        near = level_at(z, turn - 1, levels) if turn else None
        far = level_at(z, turn, levels) if turn < levels else None
        for p in range(2):
            if turn < levels:
                if 0 < turn < levels - 1:
                    z_copy(0, far, p).wait_recv()
                    z_pass(far, p)
                elif turn:

                    @pl.when(at_end)
                    def _():
                        z_copy(0, far, p).wait_recv()

                n = turn * 2 + p
                ref = out_ref.at[block(far, x, y), :, pieces[p]]
                x_copies.append(start_send(ref, ref, xs.at[n], xr.at[n], x_peer))
                y_copies.append(start_send(ref, ref, ys.at[n], yr.at[n], y_peer))
            if turn:
                d = turn - 1
                if p == 0:
                    x_copies[d * 2].wait_recv()
                    ref = out_ref.at[block(near, 1 - x, y), :, left]
                    d_copies.append(start_send(ref, ref, ds.at[d], dr.at[d], y_peer))
                else:
                    y_copies[d * 2 + 1].wait_recv()
                    ref = out_ref.at[block(near, x, 1 - y), :, right]
                    e_copies.append(start_send(ref, ref, es.at[d], er.at[d], x_peer))
        if turn < levels:
            sent[turn].append(to_core(block(far, x, y)))
        if turn:
            x_copies[d * 2 + 1].wait_recv()
            sent[d].append(to_core(block(near, 1 - x, y)))
            y_copies[d * 2].wait_recv()
            sent[d].append(to_core(block(near, x, 1 - y)))
        if turn >= 2:
            finish(turn - 2)
            if turn == levels - 2:
                ahead = level_at(z, levels - 1, levels)

                @pl.when(jnp.logical_not(at_end))
                def _():
                    for p in range(2):
                        z_copy(0, ahead, p).wait_recv()
                        z_pass(ahead, p)

            experts_of(turn - 2)
    finish(levels - 1)
    experts_of(levels - 1)
    for copy in x_copies + y_copies + d_copies + e_copies + c_copies:
        copy.wait_send()
    for k in range(levels):
        for side, (step, there) in enumerate(z_sides):

            @pl.when(jnp.logical_and(there, (z - k) * step >= 0))
            def _():
                for p in range(2):
                    z_copy(side, k, p).wait_send()


def hidden_units(stream, norm_gain, router, expert_ids, gate, up, levels):
    sub, model = stream.shape
    experts = router.shape[1]
    width = gate.shape[2]
    slots = sub * expert_ids.shape[1] // experts
    vmem = pl.BlockSpec(memory_space=pltpu.VMEM)
    hbm = pl.BlockSpec(memory_space=pl.ANY)
    dma = pltpu.SemaphoreType.DMA
    bf16 = jnp.bfloat16
    return pl.pallas_call(
        functools.partial(
            stream_kernel, levels, sub, model, model // 2, experts, slots, width // 2
        ),
        out_shape=(
            jax.ShapeDtypeStruct((levels, 8 * slots, width), bf16),
            jax.ShapeDtypeStruct((levels, 8 * sub, 8 * slots), bf16),
            jax.ShapeDtypeStruct((levels, 8 * sub, 128), jnp.float32),
        ),
        in_specs=[vmem] * 4 + [hbm] * 2,
        out_specs=(vmem,) * 3,
        scratch_shapes=[
            pltpu.VMEM((levels * 8, sub, model + 128), bf16),
            pltpu.VMEM((model, width), bf16),
            pltpu.VMEM((model, width), bf16),
            pltpu.VMEM((8 * slots, model), bf16),
        ]
        + [dma((2, 2, levels)), dma((2, levels))]
        + [dma((levels * 2,))] * 4
        + [dma((levels,))] * 4
        + [dma((levels * 4,))] * 2
        + [dma((model // LOAD_ROWS,))] * 2,
        compiler_params=pltpu.CompilerParams(
            collective_id=1, has_side_effects=True, vmem_limit_bytes=VMEM_BYTES
        ),
    )(
        stream,
        norm_gain.reshape(1, model),
        router.T,
        expert_ids.T,
        gate,
        up,
    )


def sum_kernel(
    levels, sub, model, half, tile, hidden_ref, placing_ref, weight_ref, down_ref, stream_ref,
    out_ref, part_ref, down_w, core_in, first_in, second_in, z_in, total,
    corner_in, cs, cr, fs, fr, ss, sr, ps, zs, zr, pr, ls,
):
    def load(columns, n):
        return pltpu.make_async_copy(down_ref.at[0, :, columns], down_w.at[:, columns], ls.at[n])

    for n in range(model // tile):
        load(slice(n * tile, (n + 1) * tile), n).start()
    z, x, y, c = place_of()
    x_peer, y_peer, c_peer = at(z, 1 - x, y, c), at(z, x, 1 - y, c), at(z, x, y, 1 - c)
    announce(z, x, y, c, levels)
    f32, bf16 = jnp.float32, jnp.bfloat16
    units = levels * 2
    z_sides = ((1, z > 0), (-1, z < levels - 1))
    c_copies, stage2, stage3 = {}, {}, {}

    def place(u):
        return level_at(z, levels - 1 - u // 2, levels), u // 2, u % 2

    def terms_of(u):
        k, r, h = place(u)
        weight = jnp.concatenate([weight_ref[k]] * (tile // 128), axis=1)
        hidden = hidden_ref[k]
        placing = placing_ref[k]

        def one(j, carry):
            columns = pl.ds(pl.multiple_of(h * half + j * tile, tile), tile)
            if r == 0:
                load(columns, h * (half // tile) + j).wait()
            rows = jnp.dot(hidden, down_w[:, columns], preferred_element_type=f32).astype(bf16)
            spread = jnp.dot(placing, rows, preferred_element_type=f32)
            inner = pl.ds(pl.multiple_of(j * tile, tile), tile)
            part_ref[k, h, :, :, :, :, inner] = (
                (spread * weight).astype(bf16).reshape(2, 2, 2, sub, tile)
            )
            return carry

        lax.fori_loop(0, half // tile, one, 0)
        if u == 0:
            meet(z, levels)
        c_copies[u] = start_send(
            part_ref.at[k, h, :, :, 1 - c], core_in.at[r, h], cs.at[u], cr.at[u], c_peer
        )

    direct = {}
    inside = jnp.minimum(z * (levels - 1 - z), 1)

    def corner_copy(u, side, slot):
        k, _, h = place(u)
        if slot is None:
            slot = side * inside + 2 * (1 - inside)
        return pltpu.make_async_remote_copy(
            src_ref=part_ref.at[k, h, 1 - x, 1 - y, c],
            dst_ref=corner_in.at[slot, h],
            send_sem=ps.at[u],
            recv_sem=pr.at[slot, h],
            device_id=at(z + z_sides[side][0], x, y, c),
            device_id_type=MESH,
        )

    def corner_add(u, slot):
        k, _, h = place(u)
        corner_copy(u, 0, slot).wait_recv()
        part_ref[k, h, 1 - x, 1 - y, c] = (
            part_ref[k, h, 1 - x, 1 - y, c].astype(f32) + corner_in[slot, h].astype(f32)
        ).astype(bf16)

    def first_of(u):
        k, r, h = place(u)
        c_copies[u].wait_recv()
        for bx in range(2):
            for by in range(2):
                part_ref[k, h, bx, by, c] = (
                    part_ref[k, h, bx, by, c].astype(f32) + core_in[r, h, bx, by].astype(f32)
                ).astype(bf16)
        if r == levels - 1:
            for side, (_, outer) in enumerate(z_sides):
                pl.when(outer)(functools.partial(corner_add, u, side))
        elif r:
            if r == levels - 2:
                pl.when(inside == 1)(functools.partial(corner_add, u, 2))
            for side, (step, _) in enumerate(z_sides):

                @pl.when((k - z) * step > 0)
                def _():
                    corner_copy(u, side, side if r == levels - 2 else None).start()

            direct[u] = (
                start_send(
                    part_ref.at[k, h, 1 - x, y, c], first_in.at[r, h, 0],
                    fs.at[u], fr.at[u], x_peer,
                ),
                start_send(
                    part_ref.at[k, h, x, 1 - y, c], first_in.at[r, h, 1],
                    ss.at[u], sr.at[u], y_peer,
                ),
            )
            return
        if h:
            src, peer = part_ref.at[k, h, 1 - x, :, c], x_peer
        else:
            src, peer = part_ref.at[k, h, :, 1 - y, c], y_peer
        stage2[u] = start_send(src, first_in.at[r, h], fs.at[u], fr.at[u], peer)

    def second_of(u):
        k, r, h = place(u)
        if u not in stage2:
            return
        stage2[u].wait_recv()
        bx, by, other, peer = (x, 1 - y, 1 - y, y_peer) if h else (1 - x, y, 1 - x, x_peer)
        part_ref[k, h, bx, by, c] = (
            part_ref[k, h, bx, by, c].astype(f32) + first_in[r, h, other].astype(f32)
        ).astype(bf16)
        stage3[u] = start_send(
            part_ref.at[k, h, bx, by, c], second_in.at[r, h], ss.at[u], sr.at[u], peer
        )

    def z_copy(u, side):
        k, _, h = place(u)
        return pltpu.make_async_remote_copy(
            src_ref=part_ref.at[k, h, x, y, c],
            dst_ref=z_in.at[side, k, h],
            send_sem=zs.at[u],
            recv_sem=zr.at[side, k, h],
            device_id=at(z + z_sides[side][0], x, y, c),
            device_id_type=MESH,
        )

    def z_send(u, with_outer):
        k, _, h = place(u)
        for side, (step, outer) in enumerate(z_sides):
            right_way = (k - z) * step > 0

            @pl.when(jnp.logical_and(right_way, outer if with_outer else jnp.logical_not(outer)))
            def _():
                if with_outer:
                    z_copy(u, side).wait_recv()
                    part_ref[k, h, x, y, c] = (
                        part_ref[k, h, x, y, c].astype(f32) + z_in[side, k, h].astype(f32)
                    ).astype(bf16)
                z_copy(u, side).start()

    def third_of(u):
        k, r, h = place(u)
        value = part_ref[k, h, x, y, c].astype(f32)
        if u in direct:
            for i, copy in enumerate(direct[u]):
                copy.wait_recv()
                value = value + first_in[r, h, i].astype(f32)
        else:
            stage3[u].wait_recv()
            value = value + first_in[r, h, y if h else x].astype(f32)
            value = value + second_in[r, h].astype(f32)
        if r < levels - 1:
            part_ref[k, h, x, y, c] = value.astype(bf16)
            z_send(u, False)
        else:
            total[h] = stream_ref[:, h * half : (h + 1) * half].astype(f32) + value

    second_lag, direct_lag, third_lag = 2, 3, 5
    terms_of(0)
    for step in range(units + third_lag):
        if step < units:
            first_of(step)
        if step + 1 < units:
            terms_of(step + 1)
        if 0 <= step - second_lag < units:
            second_of(step - second_lag)
        for u in range(units):
            outer = 0 < u // 2 < levels - 1
            lag = direct_lag if outer else third_lag
            if step == u + lag:
                third_of(u)
            if u < units - 2 and step == u + lag + (2, 4, 0)[u // 2]:
                z_send(u, True)
    for u in range(units - 2, units):
        h = u % 2
        for side, (_, outer) in enumerate(z_sides):

            @pl.when(outer)
            def _():
                z_copy(u, side).wait_recv()
                total[h] += z_in[side, z, h].astype(f32)

        out_ref[:, h * half : (h + 1) * half] = total[h].astype(bf16)
    for u in range(units):
        c_copies[u].wait_send()
        for copy in direct[u] if u in direct else (stage2[u], stage3[u]):
            copy.wait_send()
        if u in direct:
            corner_copy(u, 0, 0).wait_send()
        if u < units - 2:
            z_copy(u, 0).wait_send()


def sum_terms(hidden, placing, weight, down, stream, levels):
    sub, model = stream.shape
    half = model // 2
    tile = 1024
    vmem = pl.BlockSpec(memory_space=pltpu.VMEM)
    dma = pltpu.SemaphoreType.DMA
    bf16 = jnp.bfloat16
    return pl.pallas_call(
        functools.partial(sum_kernel, levels, sub, model, half, tile),
        out_shape=jax.ShapeDtypeStruct((sub, model), bf16),
        in_specs=[vmem] * 3 + [pl.BlockSpec(memory_space=pl.ANY), vmem],
        out_specs=vmem,
        scratch_shapes=[
            pltpu.VMEM((levels, 2, 2, 2, 2, sub, half), bf16),
            pltpu.VMEM(down.shape[1:], bf16),
            pltpu.VMEM((levels, 2, 2, 2, sub, half), bf16),
            pltpu.VMEM((levels, 2, 2, sub, half), bf16),
            pltpu.VMEM((levels, 2, sub, half), bf16),
            pltpu.VMEM((2, levels, 2, sub, half), bf16),
            pltpu.VMEM((2, sub, half), jnp.float32),
            pltpu.VMEM((3, 2, sub, half), bf16),
        ]
        + [dma((levels * 2,))] * 8
        + [dma((2, levels, 2)), dma((3, 2)), dma((model // tile,))],
        compiler_params=pltpu.CompilerParams(
            collective_id=2, has_side_effects=True, vmem_limit_bytes=VMEM_BYTES
        ),
    )(hidden, placing, weight, down, stream)


def on_device(
    levels,
    queries,
    keys,
    values,
    resid_in,
    span_order,
    out_weight,
    norm_gain,
    router,
    expert_ids,
    w_gate,
    w_up,
    w_down,
):
    blocks = levels * 2
    per_block = queries.shape[0] // SPAN
    within = jnp.arange(SPAN, dtype=jnp.int32)
    positions = span_order.reshape(blocks, 1, per_block, 1) * SPAN + within
    positions = positions.astype(jnp.float32).reshape(blocks, 1, per_block * SPAN)
    stream = attend(queries, keys, values, positions, resid_in, out_weight, levels)
    hidden, placing, weight = hidden_units(
        stream, norm_gain, router, expert_ids, w_gate, w_up, levels
    )
    return sum_terms(hidden, placing, weight, w_down, stream, levels)


def solution(mesh):
    placed = (
        P("ctx", "exp"),
        P("ctx", "exp"),
        P("ctx", "exp"),
        P(("ctx", "exp"), None),
        P(),
        P("exp", None),
        P(),
        P(),
        P(("ctx", "exp"), None),
        P("exp", None, "ctx"),
        P("exp", None, "ctx"),
        P("exp", "ctx", None),
    )
    levels = mesh.shape["ctx"] // 2

    def body(queries, keys, values, resid_in, *rest):
        blocks = resid_in.size * mesh.size * 2
        small = mesh.shape["exp"] == 4 and levels == 4 and blocks * 4 <= VMEM_BYTES
        local = functools.partial(on_device, levels) if small else on_device_xla
        return local(queries, keys, values, resid_in, *rest)

    return jax.shard_map(
        body, mesh=mesh, in_specs=placed, out_specs=P(("ctx", "exp"), None), check_vma=False
    )
```

time: 160 us -> 144 us (0.900)
  matrix products: 6.9 us -> 0 us
  Pallas kernels: 144 us -> 141 us
  local copies, waits for them, and re-layouts: 4.78 us -> 2 us
  other arithmetic: 3.98 us -> 1.26 us
    dot_general x3 -> x0, matrix products: 6.9 us -> none  [the longest x1 5.67 us: on_device(): jnp.dot(attended, out_weight, preferred_element_type=jnp.float32)]
    reshape x3 -> x0, local copies, waits for them, and re-layouts: 2.41 us -> none  [the longest x1 1.17 us: on_device(): key_head_rows = all_keys.reshape(key_count, kv_heads, HEAD_SIZE)]
    sub x1 -> x0, other arithmetic: 2.27 us -> none  [on_device(): scores - row_max[..., None]]
    pallas_call x2, Pallas kernels: 91.5 us -> 89.4 us  [the longest x1 54.2 us: hidden_units(): pl.pallas_call(functools.partial(stream_kernel, levels, sub, model, model...]
where the time goes in v2:
time: 144 us
  Pallas kernels  141 us (98%)
  local copies, waits for them, and re-layouts  2 us (1%)
    pallas_call x1, Pallas kernels, hidden_units(): pl.pallas_call(functools.partial(stream_kernel, levels, sub, model, model...  54.2 us
    pallas_call x1, Pallas kernels, sum_terms(): pl.pallas_call(functools.partial(sum_kernel, levels, sub, model, half, ti...  51.4 us
    pallas_call x1, Pallas kernels, attend(): pl.pallas_call(functools.partial(attend_kernel, levels, heads, group, par...  35.2 us

profile of v2, /device:TPU:0, one launch (start us, length us, event | category | flops | bytes accessed | tf_op | source)
XLA Modules:
  0.0 144.0 jit_solution(18305299436983691021)
XLA Ops:
  0.0 0.7 broadcast_multiply_fusion
  0.7 0.1 add.31
  0.7 0.1 mul.12
  0.8 0.1 add.28
  0.9 0.1 add.29
  1.0 0.6 add_convert_fusion.pos_ref
  1.6 35.2 %shard_map.118.stream_ref = bf16[32,4096]{1,0:T(8,128)(2,1)} custom-call(bf16[128,1024]{1,0:T(8,128)(2,1)} %q_ref.1, bf16[128,256]{1,0:T(8,128)(2,1)} %k_ref.1, bf16[128,256]{1,0:T(8,128)(2,1)} %v_ref.1, f32[8,1,128]{2,1,0:T(1,128)} %add_convert_fusion.pos_ref, bf16[32,4096]{1,0:T(8,128)(2,1)} %resid_ref.1, bf16[1024,4096]{1,0:T(8,128)(2,1)} %weight_ref.1), custom_call_target="tpu_custom_call" | custom-call | tf_op jit(solution)/shard_map/pallas_call | solution.py:367
  36.8 54.2 %shard_map.119 = (bf16[4,128,1792]{2,1,0:T(8,128)(2,1)}, bf16[4,256,128]{2,1,0:T(8,128)(2,1)}, f32[4,256,128]{2,1,0:T(8,128)}) custom-call(bf16[32,4096]{1,0:T(8,128)(2,1)} %shard_map.118.stream_ref, f32[1,4096]{1,0:T(1,128)} %bitcast.4, f32[4,4096]{1,0:T(4,128)} %bitcast.3, s32[2,32]{1,0:T(2,128)} %bitcast.5, bf16[1,4096,1792]{2,1,0:T(8,128)(2,1)} %gate_ref.1, ...), custom_call_target="tpu_custom_call" | custom-call | tf_op jit(solution)/shard_map/pallas_call | solution.py:631
  91.0 51.4 %shard_map.120 = bf16[32,4096]{1,0:T(8,128)(2,1)} custom-call(bf16[4,128,1792]{2,1,0:T(8,128)(2,1)} %get-tuple-element.8.hidden_ref, bf16[4,256,128]{2,1,0:T(8,128)(2,1)} %get-tuple-element.9.placing_ref, f32[4,256,128]{2,1,0:T(8,128)} %get-tuple-element.10.weight_ref, bf16[1,1792,4096]{2,1,0:T(8,128)(2,1)} %down_ref.1, bf16[32,4096]{1,0:T(8,128)(2,1)} %shard_map.118.stream_ref), custom_call_target="tpu_custom_call" | custom-call | tf_op jit(solution)/shard_map/pallas_call | solution.py:870
  142.4 1.7 %copy.14 = bf16[32,4096]{1,0:T(8,128)(2,1)} copy(bf16[32,4096]{1,0:T(8,128)(2,1)} %shard_map.120) | data formatting | bytes 524288
  (1 shorter events, 0.0 us)

commit v3 on v2

--- a/solution.py
+++ b/solution.py
@@ -179,7 +179,7 @@
 
 
 def attend_kernel(
-    levels, heads, group, parts, q_ref, k_ref, v_ref, pos_ref, resid_ref, weight_ref, stream_ref,
+    levels, heads, group, parts, q_ref, k_ref, v_ref, order_ref, resid_ref, weight_ref, stream_ref,
     weight, k_in, v_in, stacked, top, total, mixed, attended, projected, core_in, kept, from_y,
     ws, zs, zr, xs, xr, cs, cr, ys, yr,
 ):
@@ -246,11 +246,20 @@
         for g in range(group):
             head = h * group + g
             stacked[h, g * rows : (g + 1) * rows, :] = q_ref[:, head * size : (head + 1) * size]
-    query_pos = jnp.broadcast_to(pos_ref[mine], (rows, rows)).T
+    lane = lax.broadcasted_iota(jnp.int32, (1, rows), 1)
+
+    def positions(index):
+        spans = rows // SPAN
+        span = jnp.zeros((1, rows), jnp.int32)
+        for n in range(spans):
+            span = jnp.where(lane // SPAN == n, order_ref[index * spans + n], span)
+        return (span * SPAN + lane % SPAN).astype(f32)
+
+    query_pos = jnp.broadcast_to(positions(mine), (rows, rows)).T
     scale = 1.0 / math.sqrt(size)
 
     def attend(keys, values, index, first=False):
-        allowed = (pos_ref[index] <= query_pos)[None]
+        allowed = (positions(index) <= query_pos)[None]
 
         def one(h, carry):
             columns = pl.ds(pl.multiple_of(h * size, size), size)
@@ -355,7 +364,7 @@
                     z_copy(i, side, k).wait_send()
 
 
-def attend(queries, keys, values, positions, resid_in, out_weight, levels):
+def attend(queries, keys, values, span_order, resid_in, out_weight, levels):
     rows, width = keys.shape
     sub, model = resid_in.shape
     heads = width // HEAD_SIZE
@@ -367,7 +376,8 @@
     return pl.pallas_call(
         functools.partial(attend_kernel, levels, heads, group, parts),
         out_shape=jax.ShapeDtypeStruct((sub, model), bf16),
-        in_specs=[vmem] * 5 + [pl.BlockSpec(memory_space=pl.ANY)],
+        in_specs=[vmem] * 3
+        + [pl.BlockSpec(memory_space=pltpu.SMEM), vmem, pl.BlockSpec(memory_space=pl.ANY)],
         out_specs=vmem,
         scratch_shapes=[
             pltpu.VMEM(out_weight.shape, bf16),
@@ -392,7 +402,7 @@
         compiler_params=pltpu.CompilerParams(
             collective_id=0, has_side_effects=True, vmem_limit_bytes=VMEM_BYTES
         ),
-    )(queries, keys, values, positions, resid_in, out_weight)
+    )(queries, keys, values, span_order, resid_in, out_weight)
 
 
 def stream_kernel(
@@ -549,15 +559,11 @@
             for load in loads:
                 load.wait()
 
-        def unit(j, carry):
-            columns = pl.ds(pl.multiple_of(j * tile, tile), tile)
+        for columns in (slice(0, tile), slice(tile, hidden_ref.shape[2])):
             rows = rows_ref[...]
             gate = jnp.dot(rows, gate_w[:, columns], preferred_element_type=jnp.float32)
             up = jnp.dot(rows, up_w[:, columns], preferred_element_type=jnp.float32)
             hidden_ref[k, :, columns] = (gate * jax.nn.sigmoid(gate) * up).astype(jnp.bfloat16)
-            return carry
-
-        lax.fori_loop(0, hidden_ref.shape[2] // tile, unit, 0)
 
     for turn in range(levels + 1):
         near = level_at(z, turn - 1, levels) if turn else None
@@ -630,7 +636,7 @@
     bf16 = jnp.bfloat16
     return pl.pallas_call(
         functools.partial(
-            stream_kernel, levels, sub, model, model // 2, experts, slots, width // 2
+            stream_kernel, levels, sub, model, model // 2, experts, slots, width // 512 * 256 + 256
         ),
         out_shape=(
             jax.ShapeDtypeStruct((levels, 8 * slots, width), bf16),
@@ -824,7 +830,7 @@
         else:
             total[h] = stream_ref[:, h * half : (h + 1) * half].astype(f32) + value
 
-    second_lag, direct_lag, third_lag = 2, 3, 5
+    second_lag, direct_lag, third_lag = 2, 2, 4
     terms_of(0)
     for step in range(units + third_lag):
         if step < units:
@@ -905,12 +911,7 @@
     w_up,
     w_down,
 ):
-    blocks = levels * 2
-    per_block = queries.shape[0] // SPAN
-    within = jnp.arange(SPAN, dtype=jnp.int32)
-    positions = span_order.reshape(blocks, 1, per_block, 1) * SPAN + within
-    positions = positions.astype(jnp.float32).reshape(blocks, 1, per_block * SPAN)
-    stream = attend(queries, keys, values, positions, resid_in, out_weight, levels)
+    stream = attend(queries, keys, values, span_order, resid_in, out_weight, levels)
     hidden, placing, weight = hidden_units(
         stream, norm_gain, router, expert_ids, w_gate, w_up, levels
     )

time: 144 us -> 139 us (0.965)
  Pallas kernels: 141 us -> 138 us
    pallas_call x1, Pallas kernels: 54.2 us -> 51.9 us  [hidden_units(): pl.pallas_call(functools.partial(stream_kernel, levels, sub, model, model...]
where the time goes in v3:
time: 139 us
  Pallas kernels  138 us (99%)
  local copies, waits for them, and re-layouts  1.67 us (1%)
    pallas_call x1, Pallas kernels, hidden_units(): pl.pallas_call(functools.partial(stream_kernel, levels, sub, model, model...  51.9 us
    pallas_call x1, Pallas kernels, sum_terms(): pl.pallas_call(functools.partial(sum_kernel, levels, sub, model, half, ti...  50.5 us
    pallas_call x1, Pallas kernels, attend(): pl.pallas_call(functools.partial(attend_kernel, levels, heads, group, par...  35.2 us

profile of v3, /device:TPU:0, one launch (start us, length us, event | category | flops | bytes accessed | tf_op | source)
XLA Modules:
  0.0 139.3 jit_solution(18359165291947306559)
XLA Ops:
  0.0 35.2 %shard_map.118.stream_ref = bf16[32,4096]{1,0:T(8,128)(2,1)} custom-call(bf16[128,1024]{1,0:T(8,128)(2,1)} %q_ref.1, bf16[128,256]{1,0:T(8,128)(2,1)} %k_ref.1, bf16[128,256]{1,0:T(8,128)(2,1)} %v_ref.1, s32[16]{0:T(128)} %order_ref.1, bf16[32,4096]{1,0:T(8,128)(2,1)} %resid_ref.1, bf16[1024,4096]{1,0:T(8,128)(2,1)} %weight_ref.1), custom_call_target="tpu_custom_call" | custom-call | tf_op jit(solution)/shard_map/pallas_call | solution.py:376
  35.2 51.9 %shard_map.119 = (bf16[4,128,1792]{2,1,0:T(8,128)(2,1)}, bf16[4,256,128]{2,1,0:T(8,128)(2,1)}, f32[4,256,128]{2,1,0:T(8,128)}) custom-call(bf16[32,4096]{1,0:T(8,128)(2,1)} %shard_map.118.stream_ref, f32[1,4096]{1,0:T(1,128)} %bitcast.4, f32[4,4096]{1,0:T(4,128)} %bitcast.3, s32[2,32]{1,0:T(2,128)} %bitcast.5, bf16[1,4096,1792]{2,1,0:T(8,128)(2,1)} %gate_ref.1, ...), custom_call_target="tpu_custom_call" | custom-call | tf_op jit(solution)/shard_map/pallas_call | solution.py:637
  87.1 50.5 %shard_map.120 = bf16[32,4096]{1,0:T(8,128)(2,1)} custom-call(bf16[4,128,1792]{2,1,0:T(8,128)(2,1)} %get-tuple-element.8.hidden_ref, bf16[4,256,128]{2,1,0:T(8,128)(2,1)} %get-tuple-element.9.placing_ref, f32[4,256,128]{2,1,0:T(8,128)} %get-tuple-element.10.weight_ref, bf16[1,1792,4096]{2,1,0:T(8,128)(2,1)} %down_ref.1, bf16[32,4096]{1,0:T(8,128)(2,1)} %shard_map.118.stream_ref), custom_call_target="tpu_custom_call" | custom-call | tf_op jit(solution)/shard_map/pallas_call | solution.py:876
  137.6 1.7 %copy.14 = bf16[32,4096]{1,0:T(8,128)(2,1)} copy(bf16[32,4096]{1,0:T(8,128)(2,1)} %shard_map.120) | data formatting | bytes 524288
